TPU v7x, 8 devices: a whole 2x2x1 slice. The times are simulated.
8 devices in a mesh: dp: 1 (over z), tp: 8 (over x, y, core).
Axes of the slice: x: 2, y: 2, z: 1, core: 2. Of those that a mesh axis runs over, the one named last changes fastest.
Arguments:
- x: bfloat16 [2048, 2048], P('dp')
- dy: bfloat16 [2048, 2048], P('dp')
- gate: bfloat16 [2048, 5120], P('dp', 'tp')
- up: bfloat16 [2048, 5120], P('dp', 'tp')
- w_gate: bfloat16 [2048, 5120], P(None, 'tp')
- w_up: bfloat16 [2048, 5120], P(None, 'tp')
- w_down: bfloat16 [5120, 2048], P('tp')
Outputs:
- output 1: bfloat16 [2048, 2048], P('dp')
- output 2: bfloat16 [2048, 5120], P('dp', 'tp')
- output 3: bfloat16 [2048, 5120], P('dp', 'tp')
- output 4: bfloat16 [5120, 2048], P(('dp', 'tp'))
All inputs are finite; a program needn't handle non-finite values.
Results may differ from a plain program's by a relative error of at most 0.012.
Values are sent between devices in bfloat16 or wider.
A program may use at most 2 GiB of HBM per device.

v0:
```python
import jax
import jax.numpy as jnp
from jax import lax
from jax.sharding import PartitionSpec as P


def act(gate, up):
    return jax.nn.gelu(gate) * up


def solution(mesh):
    def step(x, dy, gate, up, w_gate, w_up, w_down):
        hidden, back = jax.vjp(act, gate.astype(jnp.float32), up.astype(jnp.float32))
        d_hidden = jnp.dot(dy, w_down.T, preferred_element_type=jnp.float32)
        d_gate, d_up = (g.astype(jnp.bfloat16) for g in back(d_hidden))
        term = jnp.dot(d_gate, w_gate.T, preferred_element_type=jnp.float32) + jnp.dot(d_up, w_up.T, preferred_element_type=jnp.float32)
        dx = lax.psum(term.astype(jnp.bfloat16), "tp")
        dw_gate = jnp.dot(x.T, d_gate, preferred_element_type=jnp.float32)
        dw_up = jnp.dot(x.T, d_up, preferred_element_type=jnp.float32)
        dw_down = jnp.dot(hidden.astype(jnp.bfloat16).T, dy, preferred_element_type=jnp.float32)
        return dx, *(g.astype(jnp.bfloat16) for g in (dw_gate, dw_up, dw_down))

    tokens, columns, rows = P("dp", None), P(None, "tp"), P("tp", None)
    return jax.shard_map(
        step,
        mesh=mesh,
        in_specs=(tokens, tokens, P("dp", "tp"), P("dp", "tp"), columns, columns, rows),
        out_specs=(tokens, P("dp", "tp"), P("dp", "tp"), P(("dp", "tp"), None)),
        check_vma=False,
    )
```

profile of v0, /device:TPU:0, one launch (start us, length us, event | category | flops | bytes accessed | tf_op | source)
XLA Modules:
  0.0 181.0 jit_solution(6528359458124672466)
XLA Ops:
  7.2 0.0 copy-start
  7.2 0.0 all-reduce.2.cloned.1.call-start
  7.2 15.2 %fusion.4 = (bf16[2048,640]{1,0:T(8,128)(2,1)S(1)}, f32[2048,640]{1,0:T(8,128)}) fusion(bf16[2048,640]{1,0:T(8,128)(2,1)} %param.9, bf16[2048,640]{1,0:T(8,128)(2,1)} %param.10, bf16[2048,2048]{1,0:T(8,128)(2,1)} %param.8, bf16[640,2048]{1,0:T(8,128)(2,1)} %param.13), kind=kOutput, calls=%fused_computation.12 | convolution fusion | flops 5398855680 | bytes 24117248 | tf_op jit(solution)/shard_map/dot_general | solution.py:14
  22.5 0.0 copy-start.3
  22.5 0.0 copy-done
  22.5 0.0 copy-start.2
  22.5 9.6 %fusion.21 = f32[2048,2048]{1,0:T(8,128)} fusion(bf16[2048,640]{1,0:T(8,128)(2,1)S(1)} %get-tuple-element.8, bf16[2048,640]{1,0:T(8,128)(2,1)S(1)} %copy-done), kind=kOutput, calls=%fused_computation.32 | convolution fusion | flops 5368709120 | bytes 22020096 | tf_op jit(solution)/shard_map/dot_general | solution.py:16
  32.1 0.0 copy-done.3
  32.1 0.0 copy-done.2
  32.1 16.0 %add_convert_fusion = bf16[2048,2048]{1,0:T(8,128)(2,1)} fusion(f32[2048,2048]{1,0:T(8,128)} %fusion.21, bf16[2048,640]{1,0:T(8,128)(2,1)S(1)} %copy-done.2, f32[2048,640]{1,0:T(8,128)} %get-tuple-element.9, bf16[2048,640]{1,0:T(8,128)(2,1)} %param.9), kind=kOutput, calls=%fused_computation | convolution fusion | flops 5391515648 | bytes 35651584 | tf_op jit(solution)/shard_map/dot_general | solution.py:16
  48.1 0.0 all-reduce.2.cloned.1.call-update
  48.1 8.9 %fusion.10 = bf16[2048,640]{0,1:T(8,128)(2,1)S(1)} fusion(bf16[2048,640]{1,0:T(8,128)(2,1)} %copy-done.3, bf16[2048,2048]{1,0:T(8,128)(2,1)} %param.7), kind=kOutput, calls=%fused_computation.22 | convolution fusion | flops 5370019840 | bytes 13631488 | tf_op jit(solution)/shard_map/dot_general | solution.py:18
  57.0 2.6 %copy.11 = bf16[2048,640]{1,0:T(8,128)(2,1)} copy(bf16[2048,640]{0,1:T(8,128)(2,1)S(1)} %fusion.10) | data formatting | bytes 5242880
  59.6 11.7 %fusion.11 = bf16[2048,640]{0,1:T(8,128)(2,1)S(1)} fusion(bf16[2048,2048]{1,0:T(8,128)(2,1)} %param.7, f32[2048,640]{1,0:T(8,128)} %get-tuple-element.9, bf16[2048,640]{1,0:T(8,128)(2,1)} %param.9), kind=kOutput, calls=%fused_computation.23 | convolution fusion | flops 5384437760 | bytes 18874368 | tf_op jit(solution)/shard_map/dot_general | solution.py:19
  71.3 2.6 %copy.12 = bf16[2048,640]{1,0:T(8,128)(2,1)} copy(bf16[2048,640]{0,1:T(8,128)(2,1)S(1)} %fusion.11) | data formatting | bytes 5242880
  73.8 0.0 copy-start.1
  73.8 12.7 %convolution_convert_fusion = bf16[640,2048]{1,0:T(8,128)(2,1)} fusion(bf16[2048,2048]{1,0:T(8,128)(2,1)} %param.8, bf16[2048,640]{1,0:T(8,128)(2,1)} %param.10, bf16[2048,640]{1,0:T(8,128)(2,1)} %param.9), kind=kOutput, calls=%fused_computation.19 | convolution fusion | flops 5385748480 | bytes 16252928 | tf_op jit(solution)/shard_map/dot_general | solution.py:20
  86.5 79.2 %all-reduce.2.cloned.1.call-done = bf16[2048,2048]{1,0:T(8,128)(2,1)} async-done(((bf16[2048,2048]{1,0:T(8,128)(2,1)}), bf16[2048,2048]{1,0:T(8,128)(2,1)}) %all-reduce.2.cloned.1.call-update) | async-done | bytes 8388624 | tf_op jit(solution)/shard_map/psum | solution.py:17
  165.7 8.4 %copy.14 = bf16[2048,2048]{1,0:T(8,128)(2,1)} copy(bf16[2048,2048]{1,0:T(8,128)(2,1)} %all-reduce.2.cloned.1.call-done) | data formatting | bytes 16777216
  174.2 0.0 copy-done.1
Async XLA Ops:
  7.2 15.3 %copy-start = (bf16[2048,640]{1,0:T(8,128)(2,1)S(1)}, bf16[2048,640]{1,0:T(8,128)(2,1)}, u32[]{:S(2)}) copy-start(bf16[2048,640]{1,0:T(8,128)(2,1)} %param.11) | copy-start | bytes 7864324
  7.2 158.6 %all-reduce.2.cloned.1.call-start = ((), (), s32[]{:S(2)}) async-start(), calls=%async_computation | async-start | bytes 16777216 | tf_op jit(solution)/shard_map/psum | solution.py:17
  22.5 9.6 %copy-start.3 = (bf16[2048,640]{1,0:T(8,128)(2,1)}, bf16[2048,640]{1,0:T(8,128)(2,1)S(1)}, u32[]{:S(2)}) copy-start(bf16[2048,640]{1,0:T(8,128)(2,1)S(1)} %get-tuple-element.8) | copy-start | bytes 7864324
  22.5 9.6 %copy-start.2 = (bf16[2048,640]{1,0:T(8,128)(2,1)S(1)}, bf16[2048,640]{1,0:T(8,128)(2,1)}, u32[]{:S(2)}) copy-start(bf16[2048,640]{1,0:T(8,128)(2,1)} %param.12) | copy-start | bytes 7864324
  73.8 100.4 %copy-start.1 = (bf16[2048,640]{1,0:T(8,128)(2,1)S(1)}, bf16[2048,640]{1,0:T(8,128)(2,1)}, u32[]{:S(2)}) copy-start(bf16[2048,640]{1,0:T(8,128)(2,1)} %param.11) | copy-start | bytes 7864324
Sparse Core Ops, SparseCore 0:
  48.2 117.4 all-reduce.1
where the time goes:
time: 181 us
  waiting for transfers between devices  79.3 us (44%)
  matrix products  74.1 us (41%)
  between operations  14.1 us (8%)
  local copies, waits for them, and re-layouts  13.6 us (8%)
    psum x1, waiting for transfers between devices, step(): dx = lax.psum(term.astype(jnp.bfloat16), 'tp')  79.2 us
    dot_general x1, matrix products, step(): jnp.dot(d_up, w_up.T, preferred_element_type=jnp.float32)  16 us
    dot_general x1, matrix products, step(): d_hidden = jnp.dot(dy, w_down.T, preferred_element_type=jnp.float32)  15.2 us
    unnamed x11, local copies, waits for them, and re-layouts  13.6 us
    dot_general x1, matrix products, step(): jnp.dot(hidden.astype(jnp.bfloat16).T, dy, preferred_element_type=jnp.flo...  12.7 us
    dot_general x1, matrix products, step(): dw_up = jnp.dot(x.T, d_up, preferred_element_type=jnp.float32)  11.7 us
    dot_general x1, matrix products, step(): jnp.dot(d_gate, w_gate.T, preferred_element_type=jnp.float32)  9.59 us
    dot_general x1, matrix products, step(): dw_gate = jnp.dot(x.T, d_gate, preferred_element_type=jnp.float32)  8.89 us
  transfers between devices with their start and end apart: 1, of which 1 were waited for; matrix products, arithmetic and copies ran while one was open for 21% of the time, Pallas kernels for 0%

commit v1 on v0

v1 whole, which is shorter than its diff:
```python
import functools

import jax
import jax.numpy as jnp
from jax import lax
from jax.experimental import pallas as pl
from jax.experimental.pallas import tpu as pltpu
from jax.sharding import PartitionSpec as P

MESH = pl.DeviceIdType.MESH
BF = jnp.bfloat16
F32 = jnp.float32
T = 256
NC = 8
D = 2048
F = 640
B = 128
L2, L3, L4, L5 = 1, 4, 7, 11
C0 = 0.7978845608028654
C1 = 0.044715


def dot(a, b, dims=((1,), (0,))):
    return lax.dot_general(a, b, (dims, ((), ())), preferred_element_type=F32)


def kernel(
    x_hbm, dy_hbm, gate_hbm, up_hbm, wg_hbm, wu_hbm, wd_hbm,
    dx, dwg, dwu, dwd,
    wcat, wd, dcat, hid, dyc, gc, uc, xp, yp, dh, keep, outs,
    c1s, c1r, p1s, p1r, p2s, p2r,
    in_sem, w_sem, pan_sem,
    c1ss, c1rs, p1ss, p1rs, p2ss, p2rs, gss, grs, cfs, cfr,
):
    me = lax.axis_index("tp")
    c = lax.rem(me, 2)
    y = lax.rem(me // 2, 2)
    x = me // 4
    nx, ny, nc = me + 4 - 8 * x, me + 2 - 4 * y, me + 1 - 2 * c

    def rcopy(src, dst, ss, rs, to):
        return pltpu.make_async_remote_copy(
            src_ref=src, dst_ref=dst, send_sem=ss, recv_sem=rs, device_id={"tp": to}, device_id_type=MESH
        )

    def chunk_loads(k):
        s = lax.rem(k, 2)
        rows = pl.ds(pl.multiple_of(k * T, T), T)
        return [
            pltpu.make_async_copy(dy_hbm.at[rows], dyc.at[s], in_sem.at[0, s]),
            pltpu.make_async_copy(gate_hbm.at[rows], gc.at[s], in_sem.at[1, s]),
            pltpu.make_async_copy(up_hbm.at[rows], uc.at[s], in_sem.at[2, s]),
        ]

    def panel_loads(m):
        s = lax.rem(m, 2)
        cols = pl.ds(pl.multiple_of(m * T, T), T)
        return [
            pltpu.make_async_copy(x_hbm.at[:, cols], xp.at[s], pan_sem.at[0, s]),
            pltpu.make_async_copy(dy_hbm.at[:, cols], yp.at[s], pan_sem.at[1, s]),
        ]

    w_loads = []
    for g in range(4):
        own, kept = g % 2, g // 2
        h = c if own else 1 - c
        for ab in range(2):
            first, second = (x, y) if ab == 0 else (y, x)
            i = first if kept else 1 - first
            for jo in range(2):
                j = second if jo else 1 - second
                src = pl.ds(pl.multiple_of(h * 1024 + ab * 512 + i * 256 + j * 128, B), B)
                dst = pl.ds((g * 4 + ab * 2 + jo) * B, B)
                w_loads.append(pltpu.make_async_copy(wg_hbm.at[src], wcat.at[dst, 0:F], w_sem.at[1 + len(w_loads)]))
                w_loads.append(pltpu.make_async_copy(wu_hbm.at[src], wcat.at[dst, F : 2 * F], w_sem.at[1 + len(w_loads)]))
    wd_load = pltpu.make_async_copy(wd_hbm, wd, w_sem.at[0])

    for cp in chunk_loads(0):
        cp.start()
    wd_load.start()
    for cp in w_loads:
        cp.start()

    barrier = pltpu.get_barrier_semaphore()
    for to in (nx, ny, nc):
        pl.semaphore_signal(barrier, inc=1, device_id={"tp": to}, device_id_type=MESH)
    pl.semaphore_wait(barrier, 3)

    def piece(ref, k, ab, cx, cy, h):
        col = h * 1024 + (cx * 256 + cy * 128 if ab == 0 else 512 + cy * 256 + cx * 128)
        return ref.at[pl.ds(pl.multiple_of(k * T, T), T), pl.ds(pl.multiple_of(col, B), B)]

    def c1_copy(k, part):
        return rcopy(c1s.at[k, part], c1r.at[k, part], c1ss.at[k, part], c1rs.at[k, part], nc)

    def p1_copy(k, ab):
        return rcopy(p1s.at[k, ab], p1r.at[k, ab], p1ss.at[k, ab], p1rs.at[k, ab], ny if ab else nx)

    def p2_copy(k, ab):
        return rcopy(p2s.at[k, ab], p2r.at[k, ab], p2ss.at[k, ab], p2rs.at[k, ab], nx if ab else ny)

    def g_copy(k, ab, kind):
        far, near = (ny, nx) if ab else (nx, ny)
        if kind == 2:
            ref = piece(dx, k, ab, x, 1 - y, c) if ab == 0 else piece(dx, k, ab, 1 - x, y, c)
        else:
            ref = piece(dx, k, ab, x, y, c)
        return rcopy(ref, ref, gss.at[k, ab, kind], grs.at[k, ab, kind], near if kind == 0 else far)

    def cf_copy(k, ab, which):
        cx, cy = ((x, y), (x, 1 - y), (1 - x, y), (1 - x, 1 - y))[which]
        ref = piece(dx, k, ab, cx, cy, c)
        return rcopy(ref, ref, cfs.at[k, ab, which], cfr.at[k, ab, which], nc)

    def s1(k):
        c1_copy(k, 0).wait_recv()
        for ab in range(2):
            rows = pl.ds(ab * 256, 256)
            p1s[k, ab] = (outs[rows] + c1r[k, 0, rows].astype(F32)).astype(BF)
            p1_copy(k, ab).start()

    def s1b(k):
        c1_copy(k, 1).wait_recv()
        keep[k] = keep[k] + c1r[k, 1].astype(F32)

    def s2(k):
        for ab in range(2):
            p1_copy(k, ab).wait_recv()
            rows = pl.ds(ab * 256, B)
            p2s[k, ab] = (keep[k, rows] + p1r[k, ab, 0:B].astype(F32)).astype(BF)
            p2_copy(k, ab).start()
            rows = pl.ds(ab * 256 + B, B)
            keep[k, rows] = keep[k, rows] + p1r[k, ab, B : 2 * B].astype(F32)

    def s3(k):
        for ab in range(2):
            p2_copy(k, ab).wait_recv()
            done = (keep[k, pl.ds(ab * 256 + B, B)] + p2r[k, ab].astype(F32)).astype(BF)
            piece(dx, k, ab, x, y, c)[...] = done.T
            g_copy(k, ab, 0).start()
            g_copy(k, ab, 1).start()
            cf_copy(k, ab, 0).start()

    def s4(k):
        for ab in range(2):
            g_copy(k, ab, 0).wait_recv()
            g_copy(k, ab, 2).start()
            cf_copy(k, ab, 1 if ab == 0 else 2).start()
            g_copy(k, ab, 1).wait_recv()
            cf_copy(k, ab, 2 if ab == 0 else 1).start()

    def s5(k):
        for ab in range(2):
            g_copy(k, ab, 2).wait_recv()
            cf_copy(k, ab, 3).start()

    def exchange(k, lag, fn):
        @pl.when(jnp.logical_and(k >= lag, k < NC + lag))
        def _():
            fn(k - lag)

    def term(k, g, ref):
        cols = pl.ds(pl.multiple_of(k * T, T), T)
        ref[...] = dot(wcat[g * 512 : (g + 1) * 512], dcat[:, cols]).astype(ref.dtype)

    def phase1(k, _):
        slot = lax.rem(k, 2)
        cols = pl.ds(pl.multiple_of(k * T, T), T)
        for cp in chunk_loads(k):
            cp.wait()

        @pl.when(k < NC - 1)
        def _():
            for cp in chunk_loads(k + 1):
                cp.start()

        @pl.when(k == 0)
        def _():
            wd_load.wait()

        @pl.when(jnp.logical_and(k >= 2, k < 4))
        def _():
            for cp in panel_loads(k - 2):
                cp.start()

        dh[...] = dot(wd[...], dyc[slot], ((1,), (1,)))
        for r in range(5):
            rows = slice(r * B, (r + 1) * B)
            g = gc[slot, :, rows].T.astype(F32)
            u = uc[slot, :, rows].T.astype(F32)
            d = dh[rows]
            g2 = g * g
            t = jnp.tanh(g * (C0 + (C0 * C1) * g2))
            cdf = 0.5 + 0.5 * t
            act = g * cdf
            slope = cdf + (act * (1.0 - t)) * (C0 + (3.0 * C0 * C1) * g2)
            hid[rows, cols] = (act * u).astype(BF)
            dcat[rows, cols] = (d * u * slope).astype(BF)
            dcat[F + r * B : F + (r + 1) * B, cols] = (d * act).astype(BF)

        for g in range(4):

            @pl.when(k == 0)
            def _():
                for cp in w_loads[g * 8 : (g + 1) * 8]:
                    cp.wait()

            if g == 0:
                term(k, 0, c1s.at[k, 0])
                c1_copy(k, 0).start()
            elif g == 1:
                term(k, 1, outs)
            elif g == 2:
                term(k, 2, c1s.at[k, 1])
                c1_copy(k, 1).start()
                s1(k)
            else:
                term(k, 3, keep.at[k])
                s1b(k)
        exchange(k, L2, s2)
        exchange(k, L3, s3)
        exchange(k, L4, s4)
        exchange(k, L5, s5)
        return 0

    lax.fori_loop(0, NC, phase1, 0)

    def phase2(m, _):
        slot = lax.rem(m, 2)
        k = NC + m
        at = pl.ds(pl.multiple_of(m * T, T), T)
        for cp in panel_loads(m):
            cp.wait()
        dwg[at] = dot(dcat[0:F], xp[slot]).astype(BF).T
        exchange(k, L2, s2)
        exchange(k, L3, s3)
        dwu[at] = dot(dcat[F : 2 * F], xp[slot]).astype(BF).T
        exchange(k, L4, s4)
        dwd[:, at] = dot(hid[...], yp[slot]).astype(BF)

        @pl.when(m < NC - 2)
        def _():
            for cp in panel_loads(m + 2):
                cp.start()

        exchange(k, L5, s5)
        return 0

    lax.fori_loop(0, NC, phase2, 0)

    def phase3(k, _):
        exchange(k, L4, s4)
        exchange(k, L5, s5)
        return 0

    lax.fori_loop(2 * NC, NC + L5, phase3, 0)

    def finish(k, _):
        for i in range(2):
            c1_copy(k, i).wait_send()
            p1_copy(k, i).wait_send()
            p2_copy(k, i).wait_send()
            for kind in range(3):
                g_copy(k, i, kind).wait_send()
            for which in range(4):
                cf_copy(k, i, which).wait()
        return 0

    lax.fori_loop(0, NC, finish, 0)


def write_out(dx, dwg, dwu, dwd, dx_o, dwg_o, dwu_o, dwd_o, sem):
    copies = []
    for src, dst, parts in ((dx, dx_o, 8), (dwg, dwg_o, 4), (dwu, dwu_o, 4), (dwd, dwd_o, 4)):
        n = src.shape[0] // parts
        for i in range(parts):
            rows = pl.ds(i * n, n)
            copies.append(pltpu.make_async_copy(src.at[rows], dst.at[rows], sem.at[len(copies)]))
    for cp in copies:
        cp.start()
    for cp in copies:
        cp.wait()


def solution(mesh):
    def step(x, dy, gate, up, w_gate, w_up, w_down):
        hbm = pl.BlockSpec(memory_space=pltpu.HBM)
        vmem = pl.BlockSpec(memory_space=pltpu.VMEM)
        shapes = ((D, D), (D, F), (D, F), (F, D))
        dma = pltpu.SemaphoreType.DMA
        args = [pltpu.with_memory_space_constraint(a, pltpu.HBM) for a in (x, dy, gate, up, w_gate, w_up, w_down)]
        results = pl.pallas_call(
            kernel,
            out_shape=tuple(pltpu.VMEM(s, BF) for s in shapes),
            in_specs=[hbm] * 7,
            out_specs=(vmem,) * 4,
            scratch_shapes=[
                pltpu.VMEM((D, 2 * F), BF),
                pltpu.VMEM((F, D), BF),
                pltpu.VMEM((2 * F, D), BF),
                pltpu.VMEM((F, D), BF),
                pltpu.VMEM((2, T, D), BF),
                pltpu.VMEM((2, T, F), BF),
                pltpu.VMEM((2, T, F), BF),
                pltpu.VMEM((2, D, T), BF),
                pltpu.VMEM((2, D, T), BF),
                pltpu.VMEM((F, T), F32),
                pltpu.VMEM((NC, 512, T), F32),
                pltpu.VMEM((512, T), F32),
                pltpu.VMEM((NC, 2, 512, T), BF),
                pltpu.VMEM((NC, 2, 512, T), BF),
                pltpu.VMEM((NC, 2, 256, T), BF),
                pltpu.VMEM((NC, 2, 256, T), BF),
                pltpu.VMEM((NC, 2, 128, T), BF),
                pltpu.VMEM((NC, 2, 128, T), BF),
                dma((3, 2)),
                dma((33,)),
                dma((2, 2)),
                dma((NC, 2)),
                dma((NC, 2)),
                dma((NC, 2)),
                dma((NC, 2)),
                dma((NC, 2)),
                dma((NC, 2)),
                dma((NC, 2, 3)),
                dma((NC, 2, 3)),
                dma((NC, 2, 4)),
                dma((NC, 2, 4)),
            ],
            compiler_params=pltpu.CompilerParams(
                collective_id=0, has_side_effects=True, vmem_limit_bytes=48 * 2**20
            ),
        )(*args)
        return pl.pallas_call(
            write_out,
            out_shape=tuple(jax.ShapeDtypeStruct(s, BF) for s in shapes),
            in_specs=[vmem] * 4,
            out_specs=(hbm,) * 4,
            scratch_shapes=[dma((20,))],
            compiler_params=pltpu.CompilerParams(vmem_limit_bytes=2**20),
        )(*results)

    tokens, columns, rows = P("dp", None), P(None, "tp"), P("tp", None)
    return jax.shard_map(
        step,
        mesh=mesh,
        in_specs=(tokens, tokens, P("dp", "tp"), P("dp", "tp"), columns, columns, rows),
        out_specs=(tokens, P("dp", "tp"), P("dp", "tp"), P(("dp", "tp"), None)),
        check_vma=False,
    )
```

time: 181 us -> 103 us (0.57)
  Pallas kernels: 0 us -> 102 us
  waiting for transfers between devices: 79.3 us -> 0 us
  matrix products: 74.1 us -> 0 us
  local copies, waits for them, and re-layouts: 13.6 us -> 0 us
  between operations: 14.1 us -> 0.64 us
    pallas_call x0 -> x2, Pallas kernels: none -> 102 us  [the longest x1 96.1 us: step(): pl.pallas_call(kernel, out_shape=tuple((pltpu.VMEM(s, BF) for s in shapes...]
    psum x1 -> x0, waiting for transfers between devices: 79.2 us -> none  [step(): dx = lax.psum(term.astype(jnp.bfloat16), 'tp')]
    dot_general x6 -> x0, matrix products: 74.1 us -> none  [the longest x1 16 us: step(): jnp.dot(d_up, w_up.T, preferred_element_type=jnp.float32)]
    unnamed x11 -> x0, local copies, waits for them, and re-layouts: 13.6 us -> none
  transfers between devices with their start and end apart: 1 -> 0, of which waited for: 1 -> 0; matrix products, arithmetic and copies ran while one was open for 21% -> 0% of each run, Pallas kernels for 0% -> 0%
where the time goes in v1:
time: 103 us
  Pallas kernels  102 us (99%)
    pallas_call x1, Pallas kernels, step(): pl.pallas_call(kernel, out_shape=tuple((pltpu.VMEM(s, BF) for s in shapes...  96.1 us
    pallas_call x1, Pallas kernels, step(): pl.pallas_call(write_out, out_shape=tuple((jax.ShapeDtypeStruct(s, BF) fo...  5.82 us

profile of v1, /device:TPU:0, one launch (start us, length us, event | category | flops | bytes accessed | tf_op | source)
XLA Modules:
  0.0 102.6 jit_solution(5751744173114292019)
XLA Ops:
  0.6 96.1 %shard_map.102 = (bf16[2048,2048]{1,0:T(8,128)(2,1)S(1)}, bf16[2048,640]{1,0:T(8,128)(2,1)S(1)}, bf16[2048,640]{1,0:T(8,128)(2,1)S(1)}, bf16[640,2048]{1,0:T(8,128)(2,1)S(1)}) custom-call(bf16[2048,2048]{1,0:T(8,128)(2,1)} %x_hbm.1, bf16[2048,2048]{1,0:T(8,128)(2,1)} %dy_hbm.1, bf16[2048,640]{1,0:T(8,128)(2,1)} %gate_hbm.1, bf16[2048,640]{1,0:T(8,128)(2,1)} %up_hbm.1, ...), custom_call_target="tpu_custom_call" | custom-call | tf_op jit(solution)/shard_map/pallas_call | solution.py:292
  96.8 5.8 %shard_map.103 = (bf16[2048,2048]{1,0:T(8,128)(2,1)}, bf16[2048,640]{1,0:T(8,128)(2,1)}, bf16[2048,640]{1,0:T(8,128)(2,1)}, bf16[640,2048]{1,0:T(8,128)(2,1)}) custom-call(bf16[2048,2048]{1,0:T(8,128)(2,1)S(1)} %get-tuple-element.8.dx, bf16[2048,640]{1,0:T(8,128)(2,1)S(1)} %get-tuple-element.9.dwg, bf16[2048,640]{1,0:T(8,128)(2,1)S(1)} %get-tuple-element.10.dwu, ...), custom_call_target="tpu_custom_call" | custom-call | tf_op jit(solution)/shard_map/pallas_call | solution.py:334

commit v2 on v1

v2 whole, which is shorter than its diff:
```python
import functools

import jax
import jax.numpy as jnp
from jax import lax
from jax.experimental import pallas as pl
from jax.experimental.pallas import tpu as pltpu
from jax.sharding import PartitionSpec as P

MESH = pl.DeviceIdType.MESH
BF = jnp.bfloat16
F32 = jnp.float32
T = 256
NC = 8
D = 2048
F = 640
B = 128
L2, L3, L4, L5 = 1, 4, 7, 11
C0 = 0.7978845608028654
C1 = 0.044715


def dot(a, b, dims=((1,), (0,))):
    return lax.dot_general(a, b, (dims, ((), ())), preferred_element_type=F32)


def kernel(
    x_hbm, dy_hbm, gate_hbm, up_hbm, wg_hbm, wu_hbm, wd_hbm,
    dx, dwg, dwu, dwd,
    wcat, wd, dcat, hid, dyc, guc, pan, dh, keep, outs,
    c1s, c1r, p1s, p1r, p2s, p2r,
    dy_sem, gu_sem, wd_sem, w_sem, pan_sem,
    c1_sem, p1_sem, p2_sem, g01_sem, g2_sem, cf_sem, sent,
):
    me = lax.axis_index("tp")
    c = lax.rem(me, 2)
    y = lax.rem(me // 2, 2)
    x = me // 4
    nx, ny, nc = me + 4 - 8 * x, me + 2 - 4 * y, me + 1 - 2 * c

    barrier = pltpu.get_barrier_semaphore()
    for to in (nx, ny, nc):
        pl.semaphore_signal(barrier, inc=1, device_id={"tp": to}, device_id_type=MESH)

    def rcopy(src, dst, ss, rs, to):
        return pltpu.make_async_remote_copy(
            src_ref=src, dst_ref=dst, send_sem=ss, recv_sem=rs, device_id={"tp": to}, device_id_type=MESH
        )

    def take(ref, sem):
        pltpu.make_async_copy(ref, ref, sem).wait()

    def load_gu(k, s):
        rows = pl.ds(pl.multiple_of(k * T, T), T)
        pltpu.make_async_copy(gate_hbm.at[rows], guc.at[s, 0], gu_sem.at[s]).start()
        pltpu.make_async_copy(up_hbm.at[rows], guc.at[s, 1], gu_sem.at[s]).start()

    def load_chunk(k, s):
        rows = pl.ds(pl.multiple_of(k * T, T), T)
        pltpu.make_async_copy(dy_hbm.at[rows], dyc.at[s], dy_sem.at[s]).start()
        load_gu(k, s)

    def load_panel(m, s):
        cols = pl.ds(pl.multiple_of(m * T, T), T)
        pltpu.make_async_copy(x_hbm.at[:, cols], pan.at[s, 0], pan_sem.at[s]).start()
        pltpu.make_async_copy(dy_hbm.at[:, cols], pan.at[s, 1], pan_sem.at[s]).start()

    def load_w(g):
        own, kept = g % 2, g // 2
        h = c if own else 1 - c
        for ab in range(2):
            first, second = (x, y) if ab == 0 else (y, x)
            i = first if kept else 1 - first
            for jo in range(2):
                j = second if jo else 1 - second
                src = pl.ds(pl.multiple_of(h * 1024 + ab * 512 + i * 256 + j * 128, B), B)
                dst = pl.ds((g * 4 + ab * 2 + jo) * B, B)
                pltpu.make_async_copy(wg_hbm.at[src], wcat.at[dst, 0:F], w_sem.at[g]).start()
                pltpu.make_async_copy(wu_hbm.at[src], wcat.at[dst, F : 2 * F], w_sem.at[g]).start()

    def piece(ref, k, ab, cx, cy, h):
        col = h * 1024 + (cx * 256 + cy * 128 if ab == 0 else 512 + cy * 256 + cx * 128)
        return ref.at[pl.ds(pl.multiple_of(k * T, T), T), pl.ds(pl.multiple_of(col, B), B)]

    def c1_send(k, part):
        rcopy(c1s.at[k, part], c1r.at[k, part], sent.at[0], c1_sem.at[k, part], nc).start()

    def g_send(k, ab, kind):
        far, near = (ny, nx) if ab else (nx, ny)
        if kind == 2:
            ref = piece(dx, k, ab, x, 1 - y, c) if ab == 0 else piece(dx, k, ab, 1 - x, y, c)
        else:
            ref = piece(dx, k, ab, x, y, c)
        rcopy(ref, ref, sent.at[3], (g2_sem if kind == 2 else g01_sem).at[k], near if kind == 0 else far).start()

    def cf_send(k, ab, which):
        cx, cy = ((x, y), (x, 1 - y), (1 - x, y), (1 - x, 1 - y))[which]
        ref = piece(dx, k, ab, cx, cy, c)
        rcopy(ref, ref, sent.at[4], cf_sem, nc).start()

    @jax.named_scope("s1")
    def s1(k):
        take(c1r.at[k, 0], c1_sem.at[k, 0])
        for ab in range(2):
            rows = pl.ds(ab * 256, 256)
            p1s[k, ab] = (outs[rows] + c1r[k, 0, rows].astype(F32)).astype(BF)
            rcopy(p1s.at[k, ab], p1r.at[k, ab], sent.at[1], p1_sem.at[k], ny if ab else nx).start()

    @jax.named_scope("s1b")
    def s1b(k):
        take(c1r.at[k, 1], c1_sem.at[k, 1])
        keep[k] = keep[k] + c1r[k, 1].astype(F32)

    @jax.named_scope("s2")
    def s2(k):
        take(p1r.at[k], p1_sem.at[k])
        for ab in range(2):
            rows = pl.ds(ab * 256, B)
            p2s[k, ab] = (keep[k, rows] + p1r[k, ab, 0:B].astype(F32)).astype(BF)
            rcopy(p2s.at[k, ab], p2r.at[k, ab], sent.at[2], p2_sem.at[k], nx if ab else ny).start()
        for ab in range(2):
            rows = pl.ds(ab * 256 + B, B)
            keep[k, rows] = keep[k, rows] + p1r[k, ab, B : 2 * B].astype(F32)

    @jax.named_scope("s3")
    def s3(k):
        take(p2r.at[k], p2_sem.at[k])
        for ab in range(2):
            done = (keep[k, pl.ds(ab * 256 + B, B)] + p2r[k, ab].astype(F32)).astype(BF)
            piece(dx, k, ab, x, y, c)[...] = done.T
            g_send(k, ab, 0)
            g_send(k, ab, 1)
            cf_send(k, ab, 0)

    @jax.named_scope("s4")
    def s4(k):
        take(p1r.at[k], g01_sem.at[k])
        for ab in range(2):
            g_send(k, ab, 2)
            cf_send(k, ab, 1)
            cf_send(k, ab, 2)

    @jax.named_scope("s5")
    def s5(k):
        take(p2r.at[k], g2_sem.at[k])
        for ab in range(2):
            cf_send(k, ab, 3)

    def exchange(k, lag, fn):
        @pl.when(jnp.logical_and(k >= lag, k < NC + lag))
        def _():
            fn(k - lag)

    @jax.named_scope("ew")
    def gates(k, slot):
        cols = pl.ds(pl.multiple_of(k * T, T), T)
        for r in range(5):
            rows = slice(r * B, (r + 1) * B)
            g = guc[slot, 0, :, rows].T.astype(F32)
            u = guc[slot, 1, :, rows].T.astype(F32)
            d = dh[rows]
            g2 = g * g
            t = jnp.tanh(g * (C0 + (C0 * C1) * g2))
            cdf = 0.5 + 0.5 * t
            act = g * cdf
            slope = cdf + (act * (1.0 - t)) * (C0 + (3.0 * C0 * C1) * g2)
            hid[rows, cols] = (act * u).astype(BF)
            dcat[rows, cols] = (d * u * slope).astype(BF)
            dcat[F + r * B : F + (r + 1) * B, cols] = (d * act).astype(BF)

    def halves(n):
        return [slice(i * n // 2, (i + 1) * n // 2) for i in range(2)]

    @jax.named_scope("term")
    def term(k, g, ref):
        cols = pl.ds(pl.multiple_of(k * T, T), T)
        for r in halves(512):
            ref[r] = dot(wcat[g * 512 + r.start : g * 512 + r.stop], dcat[:, cols]).astype(ref.dtype)

    for i, d in enumerate(halves(D)):
        pltpu.make_async_copy(wd_hbm.at[:, d], wd.at[:, d], wd_sem.at[i]).start()
        pltpu.make_async_copy(dy_hbm.at[0:T, d], dyc.at[0, :, d], dy_sem.at[i]).start()
    load_gu(0, 0)
    for i, d in enumerate(halves(D)):
        with jax.named_scope("load"):
            take(wd.at[:, d], wd_sem.at[i])
            take(dyc.at[0, :, d], dy_sem.at[i])
        for g in ((0, 1), (2, 3))[i]:
            load_w(g)
        if i:
            load_chunk(1, 1)
        with jax.named_scope("dh"):
            for r in halves(F):
                part = dot(wd[r, d], dyc[0, :, d], ((1,), (1,)))
                dh[r] = dh[r] + part if i else part
    take(guc.at[0], gu_sem.at[0])
    gates(0, 0)
    with jax.named_scope("bar"):
        pl.semaphore_wait(barrier, 3)

    def phase1(k, _):
        for g, ref in enumerate((c1s.at[k, 0], outs, c1s.at[k, 1], keep.at[k])):

            @pl.when(k == 0)
            def _():
                take(wcat.at[g * 512 : (g + 1) * 512], w_sem.at[g])

            term(k, g, ref)
            if g == 0:
                c1_send(k, 0)
            if g == 2:
                c1_send(k, 1)
        s1(k)

        @pl.when(k < NC - 1)
        def _():
            nxt = k + 1
            slot = lax.rem(nxt, 2)
            with jax.named_scope("chunkwait"):
                take(dyc.at[slot], dy_sem.at[slot])
                take(guc.at[slot], gu_sem.at[slot])

            @pl.when(nxt < NC - 1)
            def _():
                load_chunk(nxt + 1, 1 - slot)

            @pl.when(jnp.logical_and(k >= 2, k < 4))
            def _():
                load_panel(k - 2, k - 2)

            with jax.named_scope("dh"):
                for r in halves(F):
                    dh[r] = dot(wd[r], dyc[slot], ((1,), (1,)))
            gates(nxt, slot)

        s1b(k)
        exchange(k, L2, s2)
        exchange(k, L3, s3)
        exchange(k, L4, s4)
        exchange(k, L5, s5)
        return 0

    lax.fori_loop(0, NC, phase1, 0)

    def phase2(m, _):
        slot = lax.rem(m, 2)
        k = NC + m
        at = pl.ds(pl.multiple_of(m * T, T), T)
        take(pan.at[slot], pan_sem.at[slot])
        with jax.named_scope("dwg"):
            for r in halves(F):
                dwg[at, r] = dot(dcat[r], pan[slot, 0]).astype(BF).T
        exchange(k, L2, s2)
        with jax.named_scope("dwu"):
            for r in halves(F):
                dwu[at, r] = dot(dcat[F + r.start : F + r.stop], pan[slot, 0]).astype(BF).T
        exchange(k, L3, s3)
        exchange(k, L4, s4)
        with jax.named_scope("dwd"):
            for r in halves(F):
                dwd[r, at] = dot(hid[r], pan[slot, 1]).astype(BF)

        @pl.when(m < NC - 2)
        def _():
            load_panel(m + 2, slot)

        exchange(k, L5, s5)
        return 0

    lax.fori_loop(0, NC, phase2, 0)

    def phase3(k, _):
        exchange(k, L4, s4)
        exchange(k, L5, s5)
        return 0

    lax.fori_loop(2 * NC, NC + L5, phase3, 0)
    with jax.named_scope("fin"):
        for i, ref in enumerate((c1s, p1s, p2s, dx.at[0:768], dx.at[0:1024])):
            take(ref, sent.at[i])
        take(c1r, cf_sem)


def write_out(dx, dwg, dwu, dwd, dx_o, dwg_o, dwu_o, dwd_o, sem):
    copies = []
    for src, dst, parts in ((dx, dx_o, 8), (dwg, dwg_o, 4), (dwu, dwu_o, 4), (dwd, dwd_o, 4)):
        n = src.shape[0] // parts
        for i in range(parts):
            rows = pl.ds(i * n, n)
            copies.append(pltpu.make_async_copy(src.at[rows], dst.at[rows], sem.at[len(copies)]))
    for cp in copies:
        cp.start()
    for cp in copies:
        cp.wait()


def solution(mesh):
    def step(x, dy, gate, up, w_gate, w_up, w_down):
        hbm = pl.BlockSpec(memory_space=pltpu.HBM)
        vmem = pl.BlockSpec(memory_space=pltpu.VMEM)
        shapes = ((D, D), (D, F), (D, F), (F, D))
        dma = pltpu.SemaphoreType.DMA
        args = [pltpu.with_memory_space_constraint(a, pltpu.HBM) for a in (x, dy, gate, up, w_gate, w_up, w_down)]
        results = pl.pallas_call(
            kernel,
            out_shape=tuple(pltpu.VMEM(s, BF) for s in shapes),
            in_specs=[hbm] * 7,
            out_specs=(vmem,) * 4,
            scratch_shapes=[
                pltpu.VMEM((D, 2 * F), BF),
                pltpu.VMEM((F, D), BF),
                pltpu.VMEM((2 * F, D), BF),
                pltpu.VMEM((F, D), BF),
                pltpu.VMEM((2, T, D), BF),
                pltpu.VMEM((2, 2, T, F), BF),
                pltpu.VMEM((2, 2, D, T), BF),
                pltpu.VMEM((F, T), F32),
                pltpu.VMEM((NC, 512, T), F32),
                pltpu.VMEM((512, T), F32),
                pltpu.VMEM((NC, 2, 512, T), BF),
                pltpu.VMEM((NC, 2, 512, T), BF),
                pltpu.VMEM((NC, 2, 256, T), BF),
                pltpu.VMEM((NC, 2, 256, T), BF),
                pltpu.VMEM((NC, 2, 128, T), BF),
                pltpu.VMEM((NC, 2, 128, T), BF),
                dma((2,)),
                dma((2,)),
                dma((2,)),
                dma((4,)),
                dma((2,)),
                dma((NC, 2)),
                dma((NC,)),
                dma((NC,)),
                dma((NC,)),
                dma((NC,)),
                dma,
                dma((5,)),
            ],
            compiler_params=pltpu.CompilerParams(
                collective_id=0, has_side_effects=True, vmem_limit_bytes=48 * 2**20
            ),
        )(*args)
        return pl.pallas_call(
            write_out,
            out_shape=tuple(jax.ShapeDtypeStruct(s, BF) for s in shapes),
            in_specs=[vmem] * 4,
            out_specs=(hbm,) * 4,
            scratch_shapes=[dma((20,))],
            compiler_params=pltpu.CompilerParams(vmem_limit_bytes=2**20),
        )(*results)

    tokens, columns, rows = P("dp", None), P(None, "tp"), P("tp", None)
    return jax.shard_map(
        step,
        mesh=mesh,
        in_specs=(tokens, tokens, P("dp", "tp"), P("dp", "tp"), columns, columns, rows),
        out_specs=(tokens, P("dp", "tp"), P("dp", "tp"), P(("dp", "tp"), None)),
        check_vma=False,
    )
```

time: 103 us -> 85.6 us (0.83)
  Pallas kernels: 102 us -> 84.8 us
    pallas_call x1, Pallas kernels: 96.1 us -> 79 us  [step(): pl.pallas_call(kernel, out_shape=tuple((pltpu.VMEM(s, BF) for s in shapes...]
where the time goes in v2:
time: 85.6 us; the launch traced here: 85.5 us
  Pallas kernels  84.8 us (99%)
    pallas_call x1, Pallas kernels, step(): pl.pallas_call(kernel, out_shape=tuple((pltpu.VMEM(s, BF) for s in shapes...  79 us
    pallas_call x1, Pallas kernels, step(): pl.pallas_call(write_out, out_shape=tuple((jax.ShapeDtypeStruct(s, BF) fo...  5.82 us

profile of v2, /device:TPU:0, one launch (start us, length us, event | category | flops | bytes accessed | tf_op | source)
XLA Modules:
  0.0 85.5 jit_solution(5676703374196054180)
XLA Ops:
  0.6 79.0 %shard_map.102 = (bf16[2048,2048]{1,0:T(8,128)(2,1)S(1)}, bf16[2048,640]{1,0:T(8,128)(2,1)S(1)}, bf16[2048,640]{1,0:T(8,128)(2,1)S(1)}, bf16[640,2048]{1,0:T(8,128)(2,1)S(1)}) custom-call(bf16[2048,2048]{1,0:T(8,128)(2,1)} %x_hbm.1, bf16[2048,2048]{1,0:T(8,128)(2,1)} %dy_hbm.1, bf16[2048,640]{1,0:T(8,128)(2,1)} %gate_hbm.1, bf16[2048,640]{1,0:T(8,128)(2,1)} %up_hbm.1, ...), custom_call_target="tpu_custom_call" | custom-call | tf_op jit(solution)/shard_map/pallas_call | solution.py:304
  79.7 5.8 %shard_map.103 = (bf16[2048,2048]{1,0:T(8,128)(2,1)}, bf16[2048,640]{1,0:T(8,128)(2,1)}, bf16[2048,640]{1,0:T(8,128)(2,1)}, bf16[640,2048]{1,0:T(8,128)(2,1)}) custom-call(bf16[2048,2048]{1,0:T(8,128)(2,1)S(1)} %get-tuple-element.8.dx, bf16[2048,640]{1,0:T(8,128)(2,1)S(1)} %get-tuple-element.9.dwg, bf16[2048,640]{1,0:T(8,128)(2,1)S(1)} %get-tuple-element.10.dwu, ...), custom_call_target="tpu_custom_call" | custom-call | tf_op jit(solution)/shard_map/pallas_call | solution.py:343

commit v3 on v2

--- a/solution.py
+++ b/solution.py
@@ -15,7 +15,8 @@
 D = 2048
 F = 640
 B = 128
-L2, L3, L4, L5 = 1, 4, 7, 11
+L1, L2, L3, L4, L5 = 2, 2, 5, 8, 11
+VIA = NC - 1
 C0 = 0.7978845608028654
 C1 = 0.044715
 
@@ -27,16 +28,17 @@
 def kernel(
     x_hbm, dy_hbm, gate_hbm, up_hbm, wg_hbm, wu_hbm, wd_hbm,
     dx, dwg, dwu, dwd,
-    wcat, wd, dcat, hid, dyc, guc, pan, dh, keep, outs,
-    c1s, c1r, p1s, p1r, p2s, p2r,
+    wcat, wd, dcat, hid, dyc, guc, pan, dh, act_s, slope_s, keep, outs,
+    c1s, c1r, p1s, p1r, p2s, p2r, extra,
     dy_sem, gu_sem, wd_sem, w_sem, pan_sem,
-    c1_sem, p1_sem, p2_sem, g01_sem, g2_sem, cf_sem, sent,
+    c1_sem, p1_sem, p2_sem, cf_sem, sent, extra_sem,
 ):
     me = lax.axis_index("tp")
     c = lax.rem(me, 2)
     y = lax.rem(me // 2, 2)
     x = me // 4
     nx, ny, nc = me + 4 - 8 * x, me + 2 - 4 * y, me + 1 - 2 * c
+    first_chip, last_chip = x + y == 0, x + y == 2
 
     barrier = pltpu.get_barrier_semaphore()
     for to in (nx, ny, nc):
@@ -74,7 +76,7 @@
             for jo in range(2):
                 j = second if jo else 1 - second
                 src = pl.ds(pl.multiple_of(h * 1024 + ab * 512 + i * 256 + j * 128, B), B)
-                dst = pl.ds((g * 4 + ab * 2 + jo) * B, B)
+                dst = pl.ds((g * 4 + jo * 2 + ab) * B, B)
                 pltpu.make_async_copy(wg_hbm.at[src], wcat.at[dst, 0:F], w_sem.at[g]).start()
                 pltpu.make_async_copy(wu_hbm.at[src], wcat.at[dst, F : 2 * F], w_sem.at[g]).start()
 
@@ -82,8 +84,11 @@
         col = h * 1024 + (cx * 256 + cy * 128 if ab == 0 else 512 + cy * 256 + cx * 128)
         return ref.at[pl.ds(pl.multiple_of(k * T, T), T), pl.ds(pl.multiple_of(col, B), B)]
 
+    def c1_part(ref, k, part):
+        return ref.at[k, 1] if part == 2 else ref.at[k, 0, pl.ds(part * 256, 256)]
+
     def c1_send(k, part):
-        rcopy(c1s.at[k, part], c1r.at[k, part], sent.at[0], c1_sem.at[k, part], nc).start()
+        rcopy(c1_part(c1s, k, part), c1_part(c1r, k, part), sent.at[0], c1_sem.at[lax.rem(k, 4), part], nc).start()
 
     def g_send(k, ab, kind):
         far, near = (ny, nx) if ab else (nx, ny)
@@ -91,42 +96,80 @@
             ref = piece(dx, k, ab, x, 1 - y, c) if ab == 0 else piece(dx, k, ab, 1 - x, y, c)
         else:
             ref = piece(dx, k, ab, x, y, c)
-        rcopy(ref, ref, sent.at[3], (g2_sem if kind == 2 else g01_sem).at[k], near if kind == 0 else far).start()
+        rcopy(ref, ref, sent.at[3], (p2_sem if kind == 2 else p1_sem).at[k], near if kind == 0 else far).start()
 
     def cf_send(k, ab, which):
         cx, cy = ((x, y), (x, 1 - y), (1 - x, y), (1 - x, 1 - y))[which]
         ref = piece(dx, k, ab, cx, cy, c)
         rcopy(ref, ref, sent.at[4], cf_sem, nc).start()
 
-    @jax.named_scope("s1")
-    def s1(k):
-        take(c1r.at[k, 0], c1_sem.at[k, 0])
-        for ab in range(2):
-            rows = pl.ds(ab * 256, 256)
-            p1s[k, ab] = (outs[rows] + c1r[k, 0, rows].astype(F32)).astype(BF)
-            rcopy(p1s.at[k, ab], p1r.at[k, ab], sent.at[1], p1_sem.at[k], ny if ab else nx).start()
-
-    @jax.named_scope("s1b")
-    def s1b(k):
-        take(c1r.at[k, 1], c1_sem.at[k, 1])
-        keep[k] = keep[k] + c1r[k, 1].astype(F32)
-
-    @jax.named_scope("s2")
+    def s1(k, jo):
+        with jax.named_scope("s1"):
+            take(c1_part(c1r, k, jo), c1_sem.at[lax.rem(k, 4), jo])
+        for ab in range(2):
+            rows = pl.ds(jo * 256 + ab * B, B)
+            p1s[k, jo, ab] = (outs[rows] + c1r[k, 0, rows].astype(F32)).astype(BF)
+            across, other = (ny, nx) if ab else (nx, ny)
+            plain = rcopy(p1s.at[k, jo, ab], p1r.at[k, jo, ab], sent.at[1], p1_sem.at[k], across)
+            if jo:
+                skip = jnp.logical_and(k == VIA, last_chip)
+            else:
+                skip = jnp.logical_and(k == VIA, jnp.logical_and(x + y == 1, (y if ab else x) == 1))
+
+                @pl.when(skip)
+                def _():
+                    rcopy(p1s.at[k, jo, ab], extra.at[ab], sent.at[1], extra_sem, other).start()
+
+            pl.when(jnp.logical_not(skip))(plain.start)
+
+    def s1_late():
+        @pl.when(last_chip)
+        def _():
+            with jax.named_scope("late"):
+                take(extra, extra_sem)
+            for ab in range(2):
+                rows = pl.ds(256 + ab * B, B)
+                total = outs[rows] + c1r[VIA, 0, rows].astype(F32) + extra[ab].astype(F32)
+                p1s[VIA, 1, ab] = total.astype(BF)
+                rcopy(
+                    p1s.at[VIA, 1, ab], p1r.at[VIA, 1, ab], sent.at[1], p1_sem.at[VIA], ny if ab else nx
+                ).start()
+
     def s2(k):
-        take(p1r.at[k], p1_sem.at[k])
-        for ab in range(2):
-            rows = pl.ds(ab * 256, B)
-            p2s[k, ab] = (keep[k, rows] + p1r[k, ab, 0:B].astype(F32)).astype(BF)
+        with jax.named_scope("s2"):
+            take(c1r.at[k, 1], c1_sem.at[lax.rem(k, 4), 2])
+        alone = jnp.logical_and(k == VIA, first_chip)
+
+        def total(jo, ab):
+            rows = pl.ds(jo * 256 + ab * B, B)
+            return keep[k, rows] + c1r[k, 1, rows].astype(F32)
+
+        def send(ab):
             rcopy(p2s.at[k, ab], p2r.at[k, ab], sent.at[2], p2_sem.at[k], nx if ab else ny).start()
-        for ab in range(2):
-            rows = pl.ds(ab * 256 + B, B)
-            keep[k, rows] = keep[k, rows] + p1r[k, ab, B : 2 * B].astype(F32)
+
+        @pl.when(alone)
+        def _():
+            take(p1r.at[k, 1], p1_sem.at[k])
+            for ab in range(2):
+                p2s[k, ab] = total(0, ab).astype(BF)
+                send(ab)
+
+        @pl.when(jnp.logical_not(alone))
+        def _():
+            with jax.named_scope("s2"):
+                take(p1r.at[k], p1_sem.at[k])
+            for ab in range(2):
+                p2s[k, ab] = (total(0, ab) + p1r[k, 0, ab].astype(F32)).astype(BF)
+                send(ab)
+
+        for ab in range(2):
+            keep[k, pl.ds(256 + ab * B, B)] = total(1, ab) + p1r[k, 1, ab].astype(F32)
 
     @jax.named_scope("s3")
     def s3(k):
         take(p2r.at[k], p2_sem.at[k])
         for ab in range(2):
-            done = (keep[k, pl.ds(ab * 256 + B, B)] + p2r[k, ab].astype(F32)).astype(BF)
+            done = (keep[k, pl.ds(256 + ab * B, B)] + p2r[k, ab].astype(F32)).astype(BF)
             piece(dx, k, ab, x, y, c)[...] = done.T
             g_send(k, ab, 0)
             g_send(k, ab, 1)
@@ -134,7 +177,7 @@
 
     @jax.named_scope("s4")
     def s4(k):
-        take(p1r.at[k], g01_sem.at[k])
+        take(p1r.at[k], p1_sem.at[k])
         for ab in range(2):
             g_send(k, ab, 2)
             cf_send(k, ab, 1)
@@ -142,7 +185,7 @@
 
     @jax.named_scope("s5")
     def s5(k):
-        take(p2r.at[k], g2_sem.at[k])
+        take(p2r.at[k], p2_sem.at[k])
         for ab in range(2):
             cf_send(k, ab, 3)
 
@@ -151,75 +194,126 @@
         def _():
             fn(k - lag)
 
-    @jax.named_scope("ew")
     def gates(k, slot):
         cols = pl.ds(pl.multiple_of(k * T, T), T)
         for r in range(5):
             rows = slice(r * B, (r + 1) * B)
             g = guc[slot, 0, :, rows].T.astype(F32)
             u = guc[slot, 1, :, rows].T.astype(F32)
-            d = dh[rows]
             g2 = g * g
             t = jnp.tanh(g * (C0 + (C0 * C1) * g2))
             cdf = 0.5 + 0.5 * t
             act = g * cdf
             slope = cdf + (act * (1.0 - t)) * (C0 + (3.0 * C0 * C1) * g2)
             hid[rows, cols] = (act * u).astype(BF)
-            dcat[rows, cols] = (d * u * slope).astype(BF)
-            dcat[F + r * B : F + (r + 1) * B, cols] = (d * act).astype(BF)
+            act_s[rows] = act
+            slope_s[rows] = u * slope
+
+    def store_grads(k, r, d):
+        cols = pl.ds(pl.multiple_of(k * T, T), T)
+        dcat[r, cols] = (d * slope_s[r]).astype(BF)
+        dcat[F + r.start : F + r.stop, cols] = (d * act_s[r]).astype(BF)
 
     def halves(n):
         return [slice(i * n // 2, (i + 1) * n // 2) for i in range(2)]
 
-    @jax.named_scope("term")
-    def term(k, g, ref):
-        cols = pl.ds(pl.multiple_of(k * T, T), T)
-        for r in halves(512):
-            ref[r] = dot(wcat[g * 512 + r.start : g * 512 + r.stop], dcat[:, cols]).astype(ref.dtype)
-
-    for i, d in enumerate(halves(D)):
+    def term(k, rows):
+        return dot(wcat[rows], dcat[:, pl.ds(pl.multiple_of(k * T, T), T)])
+
+    parts = halves(D)
+
+    def load_first(i):
+        d = parts[i]
         pltpu.make_async_copy(wd_hbm.at[:, d], wd.at[:, d], wd_sem.at[i]).start()
-        pltpu.make_async_copy(dy_hbm.at[0:T, d], dyc.at[0, :, d], dy_sem.at[i]).start()
+        pltpu.make_async_copy(dy_hbm.at[0:T, d], dyc.at[0, :, d], wd_sem.at[2 + i]).start()
+
+    def grads(k, slot, i, gated=False):
+        with jax.named_scope("grads"):
+            if not i and not gated:
+                gates(k, slot)
+            for r in halves(F):
+                part = dot(wd[r, parts[i]], dyc[slot, :, parts[i]], ((1,), (1,)))
+                if i:
+                    store_grads(k, r, dh[r] + part)
+                else:
+                    dh[r] = part
+
     load_gu(0, 0)
-    for i, d in enumerate(halves(D)):
+    load_first(0)
+    pl.delay(250)
+    load_first(1)
+    pl.delay(250)
+    load_w(0)
+    with jax.named_scope("load"):
+        take(guc.at[0], gu_sem.at[0])
+    with jax.named_scope("gates"):
+        gates(0, 0)
+    for i, d in enumerate(parts):
         with jax.named_scope("load"):
             take(wd.at[:, d], wd_sem.at[i])
-            take(dyc.at[0, :, d], dy_sem.at[i])
-        for g in ((0, 1), (2, 3))[i]:
-            load_w(g)
-        if i:
+            take(dyc.at[0, :, d], wd_sem.at[2 + i])
+        if not i:
+            load_w(1)
             load_chunk(1, 1)
-        with jax.named_scope("dh"):
-            for r in halves(F):
-                part = dot(wd[r, d], dyc[0, :, d], ((1,), (1,)))
-                dh[r] = dh[r] + part if i else part
-    take(guc.at[0], gu_sem.at[0])
-    gates(0, 0)
+        grads(0, 0, i, gated=True)
+    load_w(2)
+    load_w(3)
     with jax.named_scope("bar"):
         pl.semaphore_wait(barrier, 3)
 
+    def first_use(k, g):
+        @pl.when(k == 0)
+        def _():
+            take(wcat.at[g * 512 : (g + 1) * 512], w_sem.at[g])
+
+    def keep_partner(k):
+        first_use(k, 2)
+        with jax.named_scope("keeps"):
+            for r in halves(512):
+                c1s[k, 1, r] = term(k, slice(1024 + r.start, 1024 + r.stop)).astype(BF)
+        c1_send(k, 2)
+
+    def keep_own(k):
+        first_use(k, 3)
+        with jax.named_scope("keeps"):
+            for r in halves(512):
+                keep[k, r] = term(k, slice(1536 + r.start, 1536 + r.stop))
+
     def phase1(k, _):
-        for g, ref in enumerate((c1s.at[k, 0], outs, c1s.at[k, 1], keep.at[k])):
-
-            @pl.when(k == 0)
-            def _():
-                take(wcat.at[g * 512 : (g + 1) * 512], w_sem.at[g])
-
-            term(k, g, ref)
-            if g == 0:
-                c1_send(k, 0)
-            if g == 2:
-                c1_send(k, 1)
-        s1(k)
+        first_use(k, 0)
+        for ab in range(2):
+            with jax.named_scope("termP"):
+                for i in range(2):
+                    r = slice(ab * 256 + i * 128, ab * 256 + (i + 1) * 128)
+                    c1s[k, 0, r] = term(k, r).astype(BF)
+            c1_send(k, ab)
+        first_use(k, 1)
+        with jax.named_scope("out"):
+            for r in halves(512):
+                outs[r] = term(k, slice(512 + r.start, 512 + r.stop))
+        s1(k, 0)
+
+        @pl.when(k >= L1)
+        def _():
+            keep_partner(k - L1)
+
+        nxt = k + 1
+        slot = lax.rem(nxt, 2)
 
         @pl.when(k < NC - 1)
         def _():
-            nxt = k + 1
-            slot = lax.rem(nxt, 2)
-            with jax.named_scope("chunkwait"):
-                take(dyc.at[slot], dy_sem.at[slot])
-                take(guc.at[slot], gu_sem.at[slot])
-
+            take(dyc.at[slot], dy_sem.at[slot])
+            take(guc.at[slot], gu_sem.at[slot])
+            grads(nxt, slot, 0)
+
+        s1(k, 1)
+
+        @pl.when(k >= L1)
+        def _():
+            keep_own(k - L1)
+
+        @pl.when(k < NC - 1)
+        def _():
             @pl.when(nxt < NC - 1)
             def _():
                 load_chunk(nxt + 1, 1 - slot)
@@ -228,12 +322,8 @@
             def _():
                 load_panel(k - 2, k - 2)
 
-            with jax.named_scope("dh"):
-                for r in halves(F):
-                    dh[r] = dot(wd[r], dyc[slot], ((1,), (1,)))
-            gates(nxt, slot)
-
-        s1b(k)
+            grads(nxt, slot, 1)
+
         exchange(k, L2, s2)
         exchange(k, L3, s3)
         exchange(k, L4, s4)
@@ -241,6 +331,13 @@
         return 0
 
     lax.fori_loop(0, NC, phase1, 0)
+
+    def last_keeps(k, _):
+        keep_partner(k)
+        keep_own(k)
+        return 0
+
+    lax.fori_loop(NC - L1, NC, last_keeps, 0)
 
     def phase2(m, _):
         slot = lax.rem(m, 2)
@@ -250,6 +347,7 @@
         with jax.named_scope("dwg"):
             for r in halves(F):
                 dwg[at, r] = dot(dcat[r], pan[slot, 0]).astype(BF).T
+        pl.when(m == 0)(s1_late)
         exchange(k, L2, s2)
         with jax.named_scope("dwu"):
             for r in halves(F):
@@ -283,7 +381,7 @@
 
 def write_out(dx, dwg, dwu, dwd, dx_o, dwg_o, dwu_o, dwd_o, sem):
     copies = []
-    for src, dst, parts in ((dx, dx_o, 8), (dwg, dwg_o, 4), (dwu, dwu_o, 4), (dwd, dwd_o, 4)):
+    for src, dst, parts in ((dx, dx_o, 4), (dwg, dwg_o, 2), (dwu, dwu_o, 2), (dwd, dwd_o, 2)):
         n = src.shape[0] // parts
         for i in range(parts):
             rows = pl.ds(i * n, n)
@@ -315,26 +413,28 @@
                 pltpu.VMEM((2, 2, T, F), BF),
                 pltpu.VMEM((2, 2, D, T), BF),
                 pltpu.VMEM((F, T), F32),
+                pltpu.VMEM((F, T), F32),
+                pltpu.VMEM((F, T), F32),
                 pltpu.VMEM((NC, 512, T), F32),
                 pltpu.VMEM((512, T), F32),
                 pltpu.VMEM((NC, 2, 512, T), BF),
                 pltpu.VMEM((NC, 2, 512, T), BF),
-                pltpu.VMEM((NC, 2, 256, T), BF),
-                pltpu.VMEM((NC, 2, 256, T), BF),
+                pltpu.VMEM((NC, 2, 2, B, T), BF),
+                pltpu.VMEM((NC, 2, 2, B, T), BF),
                 pltpu.VMEM((NC, 2, 128, T), BF),
                 pltpu.VMEM((NC, 2, 128, T), BF),
-                dma((2,)),
+                pltpu.VMEM((2, 128, T), BF),
                 dma((2,)),
                 dma((2,)),
                 dma((4,)),
+                dma((4,)),
                 dma((2,)),
-                dma((NC, 2)),
-                dma((NC,)),
-                dma((NC,)),
+                dma((4, 3)),
                 dma((NC,)),
                 dma((NC,)),
                 dma,
                 dma((5,)),
+                dma,
             ],
             compiler_params=pltpu.CompilerParams(
                 collective_id=0, has_side_effects=True, vmem_limit_bytes=48 * 2**20
@@ -345,7 +445,7 @@
             out_shape=tuple(jax.ShapeDtypeStruct(s, BF) for s in shapes),
             in_specs=[vmem] * 4,
             out_specs=(hbm,) * 4,
-            scratch_shapes=[dma((20,))],
+            scratch_shapes=[dma((10,))],
             compiler_params=pltpu.CompilerParams(vmem_limit_bytes=2**20),
         )(*results)
 

time: 85.6 us -> 83.6 us (0.977)
  Pallas kernels: 84.8 us -> 82.4 us
    pallas_call x1, Pallas kernels: 79 us -> 76.6 us  [step(): pl.pallas_call(kernel, out_shape=tuple((pltpu.VMEM(s, BF) for s in shapes...]
where the time goes in v3:
time: 83.6 us; the launch traced here: 83 us
  Pallas kernels  82.4 us (99%)
    pallas_call x1, Pallas kernels, step(): pl.pallas_call(kernel, out_shape=tuple((pltpu.VMEM(s, BF) for s in shapes...  76.6 us
    pallas_call x1, Pallas kernels, step(): pl.pallas_call(write_out, out_shape=tuple((jax.ShapeDtypeStruct(s, BF) fo...  5.76 us

profile of v3, /device:TPU:0, one launch (start us, length us, event | category | flops | bytes accessed | tf_op | source)
XLA Modules:
  0.0 83.0 jit_solution(127227307957518426)
XLA Ops:
  0.6 76.6 %shard_map.102 = (bf16[2048,2048]{1,0:T(8,128)(2,1)S(1)}, bf16[2048,640]{1,0:T(8,128)(2,1)S(1)}, bf16[2048,640]{1,0:T(8,128)(2,1)S(1)}, bf16[640,2048]{1,0:T(8,128)(2,1)S(1)}) custom-call(bf16[2048,2048]{1,0:T(8,128)(2,1)} %x_hbm.1, bf16[2048,2048]{1,0:T(8,128)(2,1)} %dy_hbm.1, bf16[2048,640]{1,0:T(8,128)(2,1)} %gate_hbm.1, bf16[2048,640]{1,0:T(8,128)(2,1)} %up_hbm.1, ...), custom_call_target="tpu_custom_call" | custom-call | tf_op jit(solution)/shard_map/pallas_call | solution.py:402
  77.3 5.8 %shard_map.103 = (bf16[2048,2048]{1,0:T(8,128)(2,1)}, bf16[2048,640]{1,0:T(8,128)(2,1)}, bf16[2048,640]{1,0:T(8,128)(2,1)}, bf16[640,2048]{1,0:T(8,128)(2,1)}) custom-call(bf16[2048,2048]{1,0:T(8,128)(2,1)S(1)} %get-tuple-element.8.dx, bf16[2048,640]{1,0:T(8,128)(2,1)S(1)} %get-tuple-element.9.dwg, bf16[2048,640]{1,0:T(8,128)(2,1)S(1)} %get-tuple-element.10.dwu, ...), custom_call_target="tpu_custom_call" | custom-call | tf_op jit(solution)/shard_map/pallas_call | solution.py:443

commit v4 on v3

--- a/solution.py
+++ b/solution.py
@@ -220,42 +220,43 @@
     def term(k, rows):
         return dot(wcat[rows], dcat[:, pl.ds(pl.multiple_of(k * T, T), T)])
 
-    parts = halves(D)
+    parts = (slice(0, 512), slice(512, 1280), slice(1280, D))
 
     def load_first(i):
         d = parts[i]
         pltpu.make_async_copy(wd_hbm.at[:, d], wd.at[:, d], wd_sem.at[i]).start()
-        pltpu.make_async_copy(dy_hbm.at[0:T, d], dyc.at[0, :, d], wd_sem.at[2 + i]).start()
-
-    def grads(k, slot, i, gated=False):
+        pltpu.make_async_copy(dy_hbm.at[0:T, d], dyc.at[0, :, d], wd_sem.at[3 + i]).start()
+
+    def grads(k, slot, parts, i):
         with jax.named_scope("grads"):
-            if not i and not gated:
+            if not i:
                 gates(k, slot)
             for r in halves(F):
                 part = dot(wd[r, parts[i]], dyc[slot, :, parts[i]], ((1,), (1,)))
-                if i:
-                    store_grads(k, r, dh[r] + part)
+                total = dh[r] + part if i else part
+                if i == len(parts) - 1:
+                    store_grads(k, r, total)
                 else:
-                    dh[r] = part
-
+                    dh[r] = total
+
+    load_first(0)
     load_gu(0, 0)
-    load_first(0)
     pl.delay(250)
     load_first(1)
     pl.delay(250)
+    load_first(2)
+    pl.delay(250)
     load_w(0)
-    with jax.named_scope("load"):
-        take(guc.at[0], gu_sem.at[0])
-    with jax.named_scope("gates"):
-        gates(0, 0)
     for i, d in enumerate(parts):
         with jax.named_scope("load"):
+            if not i:
+                take(guc.at[0], gu_sem.at[0])
             take(wd.at[:, d], wd_sem.at[i])
-            take(dyc.at[0, :, d], wd_sem.at[2 + i])
+            take(dyc.at[0, :, d], wd_sem.at[3 + i])
         if not i:
             load_w(1)
             load_chunk(1, 1)
-        grads(0, 0, i, gated=True)
+        grads(0, 0, parts, i)
     load_w(2)
     load_w(3)
     with jax.named_scope("bar"):
@@ -304,7 +305,7 @@
         def _():
             take(dyc.at[slot], dy_sem.at[slot])
             take(guc.at[slot], gu_sem.at[slot])
-            grads(nxt, slot, 0)
+            grads(nxt, slot, halves(D), 0)
 
         s1(k, 1)
 
@@ -322,7 +323,7 @@
             def _():
                 load_panel(k - 2, k - 2)
 
-            grads(nxt, slot, 1)
+            grads(nxt, slot, halves(D), 1)
 
         exchange(k, L2, s2)
         exchange(k, L3, s3)
@@ -426,7 +427,7 @@
                 pltpu.VMEM((2, 128, T), BF),
                 dma((2,)),
                 dma((2,)),
-                dma((4,)),
+                dma((6,)),
                 dma((4,)),
                 dma((2,)),
                 dma((4, 3)),

time: 83.6 us -> 83.4 us (level)
  no operation moved by 1% of the time
where the time goes in v4:
time: 83.4 us; the launch traced here: 82.8 us
  Pallas kernels  82.2 us (99%)
    pallas_call x1, Pallas kernels, step(): pl.pallas_call(kernel, out_shape=tuple((pltpu.VMEM(s, BF) for s in shapes...  76.4 us
    pallas_call x1, Pallas kernels, step(): pl.pallas_call(write_out, out_shape=tuple((jax.ShapeDtypeStruct(s, BF) fo...  5.76 us

profile of v4, /device:TPU:0, one launch (start us, length us, event | category | flops | bytes accessed | tf_op | source)
XLA Modules:
  0.0 82.8 jit_solution(15268714041064698544)
XLA Ops:
  0.6 76.4 %shard_map.102 = (bf16[2048,2048]{1,0:T(8,128)(2,1)S(1)}, bf16[2048,640]{1,0:T(8,128)(2,1)S(1)}, bf16[2048,640]{1,0:T(8,128)(2,1)S(1)}, bf16[640,2048]{1,0:T(8,128)(2,1)S(1)}) custom-call(bf16[2048,2048]{1,0:T(8,128)(2,1)} %x_hbm.1, bf16[2048,2048]{1,0:T(8,128)(2,1)} %dy_hbm.1, bf16[2048,640]{1,0:T(8,128)(2,1)} %gate_hbm.1, bf16[2048,640]{1,0:T(8,128)(2,1)} %up_hbm.1, ...), custom_call_target="tpu_custom_call" | custom-call | tf_op jit(solution)/shard_map/pallas_call | solution.py:403
  77.1 5.8 %shard_map.103 = (bf16[2048,2048]{1,0:T(8,128)(2,1)}, bf16[2048,640]{1,0:T(8,128)(2,1)}, bf16[2048,640]{1,0:T(8,128)(2,1)}, bf16[640,2048]{1,0:T(8,128)(2,1)}) custom-call(bf16[2048,2048]{1,0:T(8,128)(2,1)S(1)} %get-tuple-element.8.dx, bf16[2048,640]{1,0:T(8,128)(2,1)S(1)} %get-tuple-element.9.dwg, bf16[2048,640]{1,0:T(8,128)(2,1)S(1)} %get-tuple-element.10.dwu, ...), custom_call_target="tpu_custom_call" | custom-call | tf_op jit(solution)/shard_map/pallas_call | solution.py:444

commit v5 on v4

--- a/solution.py
+++ b/solution.py
@@ -17,6 +17,7 @@
 B = 128
 L1, L2, L3, L4, L5 = 2, 2, 5, 8, 11
 VIA = NC - 1
+RV = 112
 C0 = 0.7978845608028654
 C1 = 0.044715
 
@@ -30,7 +31,7 @@
     dx, dwg, dwu, dwd,
     wcat, wd, dcat, hid, dyc, guc, pan, dh, act_s, slope_s, keep, outs,
     c1s, c1r, p1s, p1r, p2s, p2r, extra,
-    dy_sem, gu_sem, wd_sem, w_sem, pan_sem,
+    in_sem, first_sem, w_sem, pan_sem,
     c1_sem, p1_sem, p2_sem, cf_sem, sent, extra_sem,
 ):
     me = lax.axis_index("tp")
@@ -52,15 +53,15 @@
     def take(ref, sem):
         pltpu.make_async_copy(ref, ref, sem).wait()
 
-    def load_gu(k, s):
+    def load_gu(k, s, sem):
         rows = pl.ds(pl.multiple_of(k * T, T), T)
-        pltpu.make_async_copy(gate_hbm.at[rows], guc.at[s, 0], gu_sem.at[s]).start()
-        pltpu.make_async_copy(up_hbm.at[rows], guc.at[s, 1], gu_sem.at[s]).start()
+        pltpu.make_async_copy(gate_hbm.at[rows], guc.at[s, 0], sem).start()
+        pltpu.make_async_copy(up_hbm.at[rows], guc.at[s, 1], sem).start()
 
     def load_chunk(k, s):
         rows = pl.ds(pl.multiple_of(k * T, T), T)
-        pltpu.make_async_copy(dy_hbm.at[rows], dyc.at[s], dy_sem.at[s]).start()
-        load_gu(k, s)
+        pltpu.make_async_copy(dy_hbm.at[rows], dyc.at[s], in_sem.at[s]).start()
+        load_gu(k, s, in_sem.at[s])
 
     def load_panel(m, s):
         cols = pl.ds(pl.multiple_of(m * T, T), T)
@@ -77,8 +78,8 @@
                 j = second if jo else 1 - second
                 src = pl.ds(pl.multiple_of(h * 1024 + ab * 512 + i * 256 + j * 128, B), B)
                 dst = pl.ds((g * 4 + jo * 2 + ab) * B, B)
-                pltpu.make_async_copy(wg_hbm.at[src], wcat.at[dst, 0:F], w_sem.at[g]).start()
-                pltpu.make_async_copy(wu_hbm.at[src], wcat.at[dst, F : 2 * F], w_sem.at[g]).start()
+                pltpu.make_async_copy(wg_hbm.at[src], wcat.at[dst, 0:F], w_sem.at[min(g, 2)]).start()
+                pltpu.make_async_copy(wu_hbm.at[src], wcat.at[dst, F : 2 * F], w_sem.at[min(g, 2)]).start()
 
     def piece(ref, k, ab, cx, cy, h):
         col = h * 1024 + (cx * 256 + cy * 128 if ab == 0 else 512 + cy * 256 + cx * 128)
@@ -87,8 +88,11 @@
     def c1_part(ref, k, part):
         return ref.at[k, 1] if part == 2 else ref.at[k, 0, pl.ds(part * 256, 256)]
 
+    def c1_slot(k, part):
+        return 4 + lax.rem(k, 4) if part == 2 else 2 * part + lax.rem(k, 2)
+
     def c1_send(k, part):
-        rcopy(c1_part(c1s, k, part), c1_part(c1r, k, part), sent.at[0], c1_sem.at[lax.rem(k, 4), part], nc).start()
+        rcopy(c1_part(c1s, k, part), c1_part(c1r, k, part), sent.at[1], c1_sem.at[c1_slot(k, part)], nc).start()
 
     def g_send(k, ab, kind):
         far, near = (ny, nx) if ab else (nx, ny)
@@ -96,21 +100,21 @@
             ref = piece(dx, k, ab, x, 1 - y, c) if ab == 0 else piece(dx, k, ab, 1 - x, y, c)
         else:
             ref = piece(dx, k, ab, x, y, c)
-        rcopy(ref, ref, sent.at[3], (p2_sem if kind == 2 else p1_sem).at[k], near if kind == 0 else far).start()
+        rcopy(ref, ref, sent.at[0], (p2_sem if kind == 2 else p1_sem).at[k], near if kind == 0 else far).start()
 
     def cf_send(k, ab, which):
         cx, cy = ((x, y), (x, 1 - y), (1 - x, y), (1 - x, 1 - y))[which]
         ref = piece(dx, k, ab, cx, cy, c)
-        rcopy(ref, ref, sent.at[4], cf_sem, nc).start()
+        rcopy(ref, ref, sent.at[1], cf_sem, nc).start()
 
     def s1(k, jo):
         with jax.named_scope("s1"):
-            take(c1_part(c1r, k, jo), c1_sem.at[lax.rem(k, 4), jo])
+            take(c1_part(c1r, k, jo), c1_sem.at[c1_slot(k, jo)])
         for ab in range(2):
             rows = pl.ds(jo * 256 + ab * B, B)
             p1s[k, jo, ab] = (outs[rows] + c1r[k, 0, rows].astype(F32)).astype(BF)
             across, other = (ny, nx) if ab else (nx, ny)
-            plain = rcopy(p1s.at[k, jo, ab], p1r.at[k, jo, ab], sent.at[1], p1_sem.at[k], across)
+            plain = rcopy(p1s.at[k, jo, ab], p1r.at[k, jo, ab], sent.at[0], p1_sem.at[k], across)
             if jo:
                 skip = jnp.logical_and(k == VIA, last_chip)
             else:
@@ -118,7 +122,11 @@
 
                 @pl.when(skip)
                 def _():
-                    rcopy(p1s.at[k, jo, ab], extra.at[ab], sent.at[1], extra_sem, other).start()
+                    part = p1s.at[k, jo, ab, pl.ds(0, RV)]
+                    rcopy(part, extra.at[ab], sent.at[0], extra_sem, other).start()
+                    rest = pl.ds(RV, B - RV)
+                    src, dst = p1s.at[k, jo, ab, rest], p1r.at[k, jo, ab, rest]
+                    rcopy(src, dst, sent.at[0], p1_sem.at[k], across).start()
 
             pl.when(jnp.logical_not(skip))(plain.start)
 
@@ -128,16 +136,16 @@
             with jax.named_scope("late"):
                 take(extra, extra_sem)
             for ab in range(2):
-                rows = pl.ds(256 + ab * B, B)
+                rows = pl.ds(256 + ab * B, RV)
                 total = outs[rows] + c1r[VIA, 0, rows].astype(F32) + extra[ab].astype(F32)
-                p1s[VIA, 1, ab] = total.astype(BF)
+                p1s[VIA, 1, ab, 0:RV] = total.astype(BF)
                 rcopy(
-                    p1s.at[VIA, 1, ab], p1r.at[VIA, 1, ab], sent.at[1], p1_sem.at[VIA], ny if ab else nx
+                    p1s.at[VIA, 1, ab], p1r.at[VIA, 1, ab], sent.at[0], p1_sem.at[VIA], ny if ab else nx
                 ).start()
 
     def s2(k):
         with jax.named_scope("s2"):
-            take(c1r.at[k, 1], c1_sem.at[lax.rem(k, 4), 2])
+            take(c1r.at[k, 1], c1_sem.at[c1_slot(k, 2)])
         alone = jnp.logical_and(k == VIA, first_chip)
 
         def total(jo, ab):
@@ -145,13 +153,15 @@
             return keep[k, rows] + c1r[k, 1, rows].astype(F32)
 
         def send(ab):
-            rcopy(p2s.at[k, ab], p2r.at[k, ab], sent.at[2], p2_sem.at[k], nx if ab else ny).start()
+            rcopy(p2s.at[k, ab], p2r.at[k, ab], sent.at[0], p2_sem.at[k], nx if ab else ny).start()
 
         @pl.when(alone)
         def _():
-            take(p1r.at[k, 1], p1_sem.at[k])
+            take(dcat.at[0 : 2 * (2 * B - RV) * T // 1024, 0:1024], p1_sem.at[k])
             for ab in range(2):
-                p2s[k, ab] = total(0, ab).astype(BF)
+                mine = total(0, ab)
+                p2s[k, ab, 0:RV] = mine[0:RV].astype(BF)
+                p2s[k, ab, RV:B] = (mine[RV:B] + p1r[k, 0, ab, RV:B].astype(F32)).astype(BF)
                 send(ab)
 
         @pl.when(jnp.logical_not(alone))
@@ -224,8 +234,8 @@
 
     def load_first(i):
         d = parts[i]
-        pltpu.make_async_copy(wd_hbm.at[:, d], wd.at[:, d], wd_sem.at[i]).start()
-        pltpu.make_async_copy(dy_hbm.at[0:T, d], dyc.at[0, :, d], wd_sem.at[3 + i]).start()
+        pltpu.make_async_copy(wd_hbm.at[:, d], wd.at[:, d], first_sem.at[i]).start()
+        pltpu.make_async_copy(dy_hbm.at[0:T, d], dyc.at[0, :, d], first_sem.at[i]).start()
 
     def grads(k, slot, parts, i):
         with jax.named_scope("grads"):
@@ -240,7 +250,7 @@
                     dh[r] = total
 
     load_first(0)
-    load_gu(0, 0)
+    load_gu(0, 0, first_sem.at[0])
     pl.delay(250)
     load_first(1)
     pl.delay(250)
@@ -249,10 +259,8 @@
     load_w(0)
     for i, d in enumerate(parts):
         with jax.named_scope("load"):
-            if not i:
-                take(guc.at[0], gu_sem.at[0])
-            take(wd.at[:, d], wd_sem.at[i])
-            take(dyc.at[0, :, d], wd_sem.at[3 + i])
+            n = (T + F) * (d.stop - d.start) + (0 if i else 2 * T * F)
+            take(dcat.at[0 : n // 1024, 0:1024], first_sem.at[i])
         if not i:
             load_w(1)
             load_chunk(1, 1)
@@ -265,7 +273,7 @@
     def first_use(k, g):
         @pl.when(k == 0)
         def _():
-            take(wcat.at[g * 512 : (g + 1) * 512], w_sem.at[g])
+            take(wcat.at[g * 512 : 2048 if g == 2 else (g + 1) * 512], w_sem.at[g])
 
     def keep_partner(k):
         first_use(k, 2)
@@ -275,7 +283,6 @@
         c1_send(k, 2)
 
     def keep_own(k):
-        first_use(k, 3)
         with jax.named_scope("keeps"):
             for r in halves(512):
                 keep[k, r] = term(k, slice(1536 + r.start, 1536 + r.stop))
@@ -303,18 +310,9 @@
 
         @pl.when(k < NC - 1)
         def _():
-            take(dyc.at[slot], dy_sem.at[slot])
-            take(guc.at[slot], gu_sem.at[slot])
-            grads(nxt, slot, halves(D), 0)
-
-        s1(k, 1)
-
-        @pl.when(k >= L1)
-        def _():
-            keep_own(k - L1)
-
-        @pl.when(k < NC - 1)
-        def _():
+            take(dcat.at[0 : (T * D + 2 * T * F) // D], in_sem.at[slot])
+            grads(nxt, slot, (slice(0, D),), 0)
+
             @pl.when(nxt < NC - 1)
             def _():
                 load_chunk(nxt + 1, 1 - slot)
@@ -323,7 +321,11 @@
             def _():
                 load_panel(k - 2, k - 2)
 
-            grads(nxt, slot, halves(D), 1)
+        s1(k, 1)
+
+        @pl.when(k >= L1)
+        def _():
+            keep_own(k - L1)
 
         exchange(k, L2, s2)
         exchange(k, L3, s3)
@@ -375,8 +377,8 @@
 
     lax.fori_loop(2 * NC, NC + L5, phase3, 0)
     with jax.named_scope("fin"):
-        for i, ref in enumerate((c1s, p1s, p2s, dx.at[0:768], dx.at[0:1024])):
-            take(ref, sent.at[i])
+        take(dx.at[0:1536], sent.at[0])
+        take(dx, sent.at[1])
         take(c1r, cf_sem)
 
 
@@ -424,17 +426,16 @@
                 pltpu.VMEM((NC, 2, 2, B, T), BF),
                 pltpu.VMEM((NC, 2, 128, T), BF),
                 pltpu.VMEM((NC, 2, 128, T), BF),
-                pltpu.VMEM((2, 128, T), BF),
+                pltpu.VMEM((2, RV, T), BF),
                 dma((2,)),
+                dma((3,)),
+                dma((3,)),
                 dma((2,)),
-                dma((6,)),
-                dma((4,)),
-                dma((2,)),
-                dma((4, 3)),
+                dma((8,)),
                 dma((NC,)),
                 dma((NC,)),
                 dma,
-                dma((5,)),
+                dma((2,)),
                 dma,
             ],
             compiler_params=pltpu.CompilerParams(

time: 83.4 us -> 83.1 us (level)
  no operation moved by 1% of the time
where the time goes in v5:
time: 83.1 us; the launch traced here: 82.9 us
  Pallas kernels  82.2 us (99%)
    pallas_call x1, Pallas kernels, step(): pl.pallas_call(kernel, out_shape=tuple((pltpu.VMEM(s, BF) for s in shapes...  76.5 us
    pallas_call x1, Pallas kernels, step(): pl.pallas_call(write_out, out_shape=tuple((jax.ShapeDtypeStruct(s, BF) fo...  5.76 us

profile of v5, /device:TPU:0, one launch (start us, length us, event | category | flops | bytes accessed | tf_op | source)
XLA Modules:
  0.0 82.9 jit_solution(13570306208274575189)
XLA Ops:
  0.6 76.5 %shard_map.102 = (bf16[2048,2048]{1,0:T(8,128)(2,1)S(1)}, bf16[2048,640]{1,0:T(8,128)(2,1)S(1)}, bf16[2048,640]{1,0:T(8,128)(2,1)S(1)}, bf16[640,2048]{1,0:T(8,128)(2,1)S(1)}) custom-call(bf16[2048,2048]{1,0:T(8,128)(2,1)} %x_hbm.1, bf16[2048,2048]{1,0:T(8,128)(2,1)} %dy_hbm.1, bf16[2048,640]{1,0:T(8,128)(2,1)} %gate_hbm.1, bf16[2048,640]{1,0:T(8,128)(2,1)} %up_hbm.1, ...), custom_call_target="tpu_custom_call" | custom-call | tf_op jit(solution)/shard_map/pallas_call | solution.py:405
  77.1 5.8 %shard_map.103 = (bf16[2048,2048]{1,0:T(8,128)(2,1)}, bf16[2048,640]{1,0:T(8,128)(2,1)}, bf16[2048,640]{1,0:T(8,128)(2,1)}, bf16[640,2048]{1,0:T(8,128)(2,1)}) custom-call(bf16[2048,2048]{1,0:T(8,128)(2,1)S(1)} %get-tuple-element.8.dx, bf16[2048,640]{1,0:T(8,128)(2,1)S(1)} %get-tuple-element.9.dwg, bf16[2048,640]{1,0:T(8,128)(2,1)S(1)} %get-tuple-element.10.dwu, ...), custom_call_target="tpu_custom_call" | custom-call | tf_op jit(solution)/shard_map/pallas_call | solution.py:445

commit v6 on v5

--- a/solution.py
+++ b/solution.py
@@ -32,7 +32,7 @@
     wcat, wd, dcat, hid, dyc, guc, pan, dh, act_s, slope_s, keep, outs,
     c1s, c1r, p1s, p1r, p2s, p2r, extra,
     in_sem, first_sem, w_sem, pan_sem,
-    c1_sem, p1_sem, p2_sem, cf_sem, sent, extra_sem,
+    c1_sem, p1_sem, p2_sem, cf_sem, sent, extra_sem, last_sem,
 ):
     me = lax.axis_index("tp")
     c = lax.rem(me, 2)
@@ -42,7 +42,7 @@
     first_chip, last_chip = x + y == 0, x + y == 2
 
     barrier = pltpu.get_barrier_semaphore()
-    for to in (nx, ny, nc):
+    for to in (nx, ny, nc, nx + 1 - 2 * c, ny + 1 - 2 * c):
         pl.semaphore_signal(barrier, inc=1, device_id={"tp": to}, device_id_type=MESH)
 
     def rcopy(src, dst, ss, rs, to):
@@ -102,10 +102,15 @@
             ref = piece(dx, k, ab, x, y, c)
         rcopy(ref, ref, sent.at[0], (p2_sem if kind == 2 else p1_sem).at[k], near if kind == 0 else far).start()
 
-    def cf_send(k, ab, which):
+    def cf_send(k, ab, which, h=c, sem=1):
         cx, cy = ((x, y), (x, 1 - y), (1 - x, y), (1 - x, 1 - y))[which]
-        ref = piece(dx, k, ab, cx, cy, c)
-        rcopy(ref, ref, sent.at[1], cf_sem, nc).start()
+        ref = piece(dx, k, ab, cx, cy, h)
+        rcopy(ref, ref, sent.at[sem], cf_sem, nc).start()
+
+    def g_send_last(ab):
+        cx, cy = (x, 1 - y) if ab == 0 else (1 - x, y)
+        ref = piece(dx, NC - 1, ab, cx, cy, c)
+        rcopy(ref, ref, sent.at[0], last_sem, (ny if ab else nx) + 1 - c).start()
 
     def s1(k, jo):
         with jax.named_scope("s1"):
@@ -189,15 +194,32 @@
     def s4(k):
         take(p1r.at[k], p1_sem.at[k])
         for ab in range(2):
-            g_send(k, ab, 2)
+
+            @pl.when(k < NC - 1)
+            def _():
+                g_send(k, ab, 2)
+
+            @pl.when(k == NC - 1)
+            def _():
+                g_send_last(ab)
+
             cf_send(k, ab, 1)
             cf_send(k, ab, 2)
 
     @jax.named_scope("s5")
     def s5(k):
-        take(p2r.at[k], p2_sem.at[k])
-        for ab in range(2):
-            cf_send(k, ab, 3)
+        @pl.when(k < NC - 1)
+        def _():
+            take(p2r.at[k], p2_sem.at[k])
+            for ab in range(2):
+                cf_send(k, ab, 3)
+
+        @pl.when(jnp.logical_and(k == NC - 1, c == 1))
+        def _():
+            take(p1r.at[k], last_sem)
+            for ab in range(2):
+                cf_send(k, ab, 3)
+                cf_send(k, ab, 3, h=0, sem=2)
 
     def exchange(k, lag, fn):
         @pl.when(jnp.logical_and(k >= lag, k < NC + lag))
@@ -268,7 +290,7 @@
     load_w(2)
     load_w(3)
     with jax.named_scope("bar"):
-        pl.semaphore_wait(barrier, 3)
+        pl.semaphore_wait(barrier, 5)
 
     def first_use(k, g):
         @pl.when(k == 0)
@@ -378,8 +400,17 @@
     lax.fori_loop(2 * NC, NC + L5, phase3, 0)
     with jax.named_scope("fin"):
         take(dx.at[0:1536], sent.at[0])
-        take(dx, sent.at[1])
-        take(c1r, cf_sem)
+
+        @pl.when(c == 0)
+        def _():
+            take(dx.at[0:2016], sent.at[1])
+            take(dx.at[0:1056], cf_sem)
+
+        @pl.when(c == 1)
+        def _():
+            take(dx, sent.at[1])
+            take(dx.at[0:32], sent.at[2])
+            take(dx.at[0:992], cf_sem)
 
 
 def write_out(dx, dwg, dwu, dwd, dx_o, dwg_o, dwu_o, dwd_o, sem):
@@ -435,7 +466,8 @@
                 dma((NC,)),
                 dma((NC,)),
                 dma,
-                dma((2,)),
+                dma((3,)),
+                dma,
                 dma,
             ],
             compiler_params=pltpu.CompilerParams(

time: 83.1 us -> 82.8 us (level)
  no operation moved by 1% of the time
where the time goes in v6:
time: 82.8 us; the launch traced here: 82.7 us
  Pallas kernels  82.1 us (99%)
    pallas_call x1, Pallas kernels, step(): pl.pallas_call(kernel, out_shape=tuple((pltpu.VMEM(s, BF) for s in shapes...  76.3 us
    pallas_call x1, Pallas kernels, step(): pl.pallas_call(write_out, out_shape=tuple((jax.ShapeDtypeStruct(s, BF) fo...  5.76 us

profile of v6, /device:TPU:0, one launch (start us, length us, event | category | flops | bytes accessed | tf_op | source)
XLA Modules:
  0.0 82.7 jit_solution(11141077684679830553)
XLA Ops:
  0.6 76.3 %shard_map.102 = (bf16[2048,2048]{1,0:T(8,128)(2,1)S(1)}, bf16[2048,640]{1,0:T(8,128)(2,1)S(1)}, bf16[2048,640]{1,0:T(8,128)(2,1)S(1)}, bf16[640,2048]{1,0:T(8,128)(2,1)S(1)}) custom-call(bf16[2048,2048]{1,0:T(8,128)(2,1)} %x_hbm.1, bf16[2048,2048]{1,0:T(8,128)(2,1)} %dy_hbm.1, bf16[2048,640]{1,0:T(8,128)(2,1)} %gate_hbm.1, bf16[2048,640]{1,0:T(8,128)(2,1)} %up_hbm.1, ...), custom_call_target="tpu_custom_call" | custom-call | tf_op jit(solution)/shard_map/pallas_call | solution.py:436
  77.0 5.8 %shard_map.103 = (bf16[2048,2048]{1,0:T(8,128)(2,1)}, bf16[2048,640]{1,0:T(8,128)(2,1)}, bf16[2048,640]{1,0:T(8,128)(2,1)}, bf16[640,2048]{1,0:T(8,128)(2,1)}) custom-call(bf16[2048,2048]{1,0:T(8,128)(2,1)S(1)} %get-tuple-element.8.dx, bf16[2048,640]{1,0:T(8,128)(2,1)S(1)} %get-tuple-element.9.dwg, bf16[2048,640]{1,0:T(8,128)(2,1)S(1)} %get-tuple-element.10.dwu, ...), custom_call_target="tpu_custom_call" | custom-call | tf_op jit(solution)/shard_map/pallas_call | solution.py:477

commit v7 on v6

--- a/solution.py
+++ b/solution.py
@@ -15,7 +15,7 @@
 D = 2048
 F = 640
 B = 128
-L1, L2, L3, L4, L5 = 2, 2, 5, 8, 11
+L1, L2, L3, L4, L5 = 2, 2, 5, 9, 12
 VIA = NC - 1
 RV = 112
 C0 = 0.7978845608028654
@@ -110,7 +110,7 @@
     def g_send_last(ab):
         cx, cy = (x, 1 - y) if ab == 0 else (1 - x, y)
         ref = piece(dx, NC - 1, ab, cx, cy, c)
-        rcopy(ref, ref, sent.at[0], last_sem, (ny if ab else nx) + 1 - c).start()
+        rcopy(ref, ref, sent.at[0], last_sem.at[ab], (ny if ab else nx) + 1 - c).start()
 
     def s1(k, jo):
         with jax.named_scope("s1"):
@@ -216,8 +216,8 @@
 
         @pl.when(jnp.logical_and(k == NC - 1, c == 1))
         def _():
-            take(p1r.at[k], last_sem)
             for ab in range(2):
+                take(p2r.at[k], last_sem.at[ab])
                 cf_send(k, ab, 3)
                 cf_send(k, ab, 3, h=0, sem=2)
 
@@ -468,7 +468,7 @@
                 dma,
                 dma((3,)),
                 dma,
-                dma,
+                dma((2,)),
             ],
             compiler_params=pltpu.CompilerParams(
                 collective_id=0, has_side_effects=True, vmem_limit_bytes=48 * 2**20

time: 82.8 us -> 82.8 us (level)
  no operation moved by 1% of the time
where the time goes in v7:
time: 82.8 us; the launch traced here: 82.7 us
  Pallas kernels  82 us (99%)
    pallas_call x1, Pallas kernels, step(): pl.pallas_call(kernel, out_shape=tuple((pltpu.VMEM(s, BF) for s in shapes...  76.3 us
    pallas_call x1, Pallas kernels, step(): pl.pallas_call(write_out, out_shape=tuple((jax.ShapeDtypeStruct(s, BF) fo...  5.76 us

profile of v7, /device:TPU:0, one launch (start us, length us, event | category | flops | bytes accessed | tf_op | source)
XLA Modules:
  0.0 82.7 jit_solution(6950647639921102008)
XLA Ops:
  0.6 76.3 %shard_map.102 = (bf16[2048,2048]{1,0:T(8,128)(2,1)S(1)}, bf16[2048,640]{1,0:T(8,128)(2,1)S(1)}, bf16[2048,640]{1,0:T(8,128)(2,1)S(1)}, bf16[640,2048]{1,0:T(8,128)(2,1)S(1)}) custom-call(bf16[2048,2048]{1,0:T(8,128)(2,1)} %x_hbm.1, bf16[2048,2048]{1,0:T(8,128)(2,1)} %dy_hbm.1, bf16[2048,640]{1,0:T(8,128)(2,1)} %gate_hbm.1, bf16[2048,640]{1,0:T(8,128)(2,1)} %up_hbm.1, ...), custom_call_target="tpu_custom_call" | custom-call | tf_op jit(solution)/shard_map/pallas_call | solution.py:436
  76.9 5.8 %shard_map.103 = (bf16[2048,2048]{1,0:T(8,128)(2,1)}, bf16[2048,640]{1,0:T(8,128)(2,1)}, bf16[2048,640]{1,0:T(8,128)(2,1)}, bf16[640,2048]{1,0:T(8,128)(2,1)}) custom-call(bf16[2048,2048]{1,0:T(8,128)(2,1)S(1)} %get-tuple-element.8.dx, bf16[2048,640]{1,0:T(8,128)(2,1)S(1)} %get-tuple-element.9.dwg, bf16[2048,640]{1,0:T(8,128)(2,1)S(1)} %get-tuple-element.10.dwu, ...), custom_call_target="tpu_custom_call" | custom-call | tf_op jit(solution)/shard_map/pallas_call | solution.py:477

commit v8 on v7

--- a/solution.py
+++ b/solution.py
@@ -41,10 +41,6 @@
     nx, ny, nc = me + 4 - 8 * x, me + 2 - 4 * y, me + 1 - 2 * c
     first_chip, last_chip = x + y == 0, x + y == 2
 
-    barrier = pltpu.get_barrier_semaphore()
-    for to in (nx, ny, nc, nx + 1 - 2 * c, ny + 1 - 2 * c):
-        pl.semaphore_signal(barrier, inc=1, device_id={"tp": to}, device_id_type=MESH)
-
     def rcopy(src, dst, ss, rs, to):
         return pltpu.make_async_remote_copy(
             src_ref=src, dst_ref=dst, send_sem=ss, recv_sem=rs, device_id={"tp": to}, device_id_type=MESH
@@ -273,6 +269,9 @@
 
     load_first(0)
     load_gu(0, 0, first_sem.at[0])
+    barrier = pltpu.get_barrier_semaphore()
+    for to in (nx, ny, nc, nx + 1 - 2 * c, ny + 1 - 2 * c):
+        pl.semaphore_signal(barrier, inc=1, device_id={"tp": to}, device_id_type=MESH)
     pl.delay(250)
     load_first(1)
     pl.delay(250)
@@ -414,16 +413,14 @@
 
 
 def write_out(dx, dwg, dwu, dwd, dx_o, dwg_o, dwu_o, dwd_o, sem):
-    copies = []
-    for src, dst, parts in ((dx, dx_o, 4), (dwg, dwg_o, 2), (dwu, dwu_o, 2), (dwd, dwd_o, 2)):
+    pairs = ((dx, dx_o, 4), (dwg, dwg_o, 2), (dwu, dwu_o, 2), (dwd, dwd_o, 2))
+    for k, (src, dst, parts) in enumerate(pairs):
         n = src.shape[0] // parts
         for i in range(parts):
             rows = pl.ds(i * n, n)
-            copies.append(pltpu.make_async_copy(src.at[rows], dst.at[rows], sem.at[len(copies)]))
-    for cp in copies:
-        cp.start()
-    for cp in copies:
-        cp.wait()
+            pltpu.make_async_copy(src.at[rows], dst.at[rows], sem.at[k]).start()
+    for k, (src, dst, _) in enumerate(pairs):
+        pltpu.make_async_copy(src, dst, sem.at[k]).wait()
 
 
 def solution(mesh):
@@ -479,7 +476,7 @@
             out_shape=tuple(jax.ShapeDtypeStruct(s, BF) for s in shapes),
             in_specs=[vmem] * 4,
             out_specs=(hbm,) * 4,
-            scratch_shapes=[dma((10,))],
+            scratch_shapes=[dma((4,))],
             compiler_params=pltpu.CompilerParams(vmem_limit_bytes=2**20),
         )(*results)
 

time: 82.8 us -> 82.7 us (level)
  no operation moved by 1% of the time
where the time goes in v8:
time: 82.7 us; the launch traced here: 82.6 us
  Pallas kernels  81.9 us (99%)
    pallas_call x1, Pallas kernels, step(): pl.pallas_call(kernel, out_shape=tuple((pltpu.VMEM(s, BF) for s in shapes...  76.2 us
    pallas_call x1, Pallas kernels, step(): pl.pallas_call(write_out, out_shape=tuple((jax.ShapeDtypeStruct(s, BF) fo...  5.7 us

profile of v8, /device:TPU:0, one launch (start us, length us, event | category | flops | bytes accessed | tf_op | source)
XLA Modules:
  0.0 82.6 jit_solution(5705980647296929657)
XLA Ops:
  0.6 76.2 %shard_map.102 = (bf16[2048,2048]{1,0:T(8,128)(2,1)S(1)}, bf16[2048,640]{1,0:T(8,128)(2,1)S(1)}, bf16[2048,640]{1,0:T(8,128)(2,1)S(1)}, bf16[640,2048]{1,0:T(8,128)(2,1)S(1)}) custom-call(bf16[2048,2048]{1,0:T(8,128)(2,1)} %x_hbm.1, bf16[2048,2048]{1,0:T(8,128)(2,1)} %dy_hbm.1, bf16[2048,640]{1,0:T(8,128)(2,1)} %gate_hbm.1, bf16[2048,640]{1,0:T(8,128)(2,1)} %up_hbm.1, ...), custom_call_target="tpu_custom_call" | custom-call | tf_op jit(solution)/shard_map/pallas_call | solution.py:433
  76.9 5.7 %shard_map.103 = (bf16[2048,2048]{1,0:T(8,128)(2,1)}, bf16[2048,640]{1,0:T(8,128)(2,1)}, bf16[2048,640]{1,0:T(8,128)(2,1)}, bf16[640,2048]{1,0:T(8,128)(2,1)}) custom-call(bf16[2048,2048]{1,0:T(8,128)(2,1)S(1)} %get-tuple-element.8.dx, bf16[2048,640]{1,0:T(8,128)(2,1)S(1)} %get-tuple-element.9.dwg, bf16[2048,640]{1,0:T(8,128)(2,1)S(1)} %get-tuple-element.10.dwu, ...), custom_call_target="tpu_custom_call" | custom-call | tf_op jit(solution)/shard_map/pallas_call | solution.py:474

commit v9 on v8

--- a/solution.py
+++ b/solution.py
@@ -31,7 +31,7 @@
     dx, dwg, dwu, dwd,
     wcat, wd, dcat, hid, dyc, guc, pan, dh, act_s, slope_s, keep, outs,
     c1s, c1r, p1s, p1r, p2s, p2r, extra,
-    in_sem, first_sem, w_sem, pan_sem,
+    in_sem, first_sem, w_sem,
     c1_sem, p1_sem, p2_sem, cf_sem, sent, extra_sem, last_sem,
 ):
     me = lax.axis_index("tp")
@@ -61,8 +61,8 @@
 
     def load_panel(m, s):
         cols = pl.ds(pl.multiple_of(m * T, T), T)
-        pltpu.make_async_copy(x_hbm.at[:, cols], pan.at[s, 0], pan_sem.at[s]).start()
-        pltpu.make_async_copy(dy_hbm.at[:, cols], pan.at[s, 1], pan_sem.at[s]).start()
+        pltpu.make_async_copy(x_hbm.at[:, cols], pan.at[s, 0], first_sem.at[s]).start()
+        pltpu.make_async_copy(dy_hbm.at[:, cols], pan.at[s, 1], first_sem.at[s]).start()
 
     def load_w(g):
         own, kept = g % 2, g // 2
@@ -367,7 +367,7 @@
         slot = lax.rem(m, 2)
         k = NC + m
         at = pl.ds(pl.multiple_of(m * T, T), T)
-        take(pan.at[slot], pan_sem.at[slot])
+        take(pan.at[slot], first_sem.at[slot])
         with jax.named_scope("dwg"):
             for r in halves(F):
                 dwg[at, r] = dot(dcat[r], pan[slot, 0]).astype(BF).T
@@ -458,7 +458,6 @@
                 dma((2,)),
                 dma((3,)),
                 dma((3,)),
-                dma((2,)),
                 dma((8,)),
                 dma((NC,)),
                 dma((NC,)),

time: 82.7 us -> 82.7 us (level)
  no operation moved by 1% of the time
where the time goes in v9:
time: 82.7 us; the launch traced here: 82.5 us
  Pallas kernels  81.9 us (99%)
    pallas_call x1, Pallas kernels, step(): pl.pallas_call(kernel, out_shape=tuple((pltpu.VMEM(s, BF) for s in shapes...  76.2 us
    pallas_call x1, Pallas kernels, step(): pl.pallas_call(write_out, out_shape=tuple((jax.ShapeDtypeStruct(s, BF) fo...  5.7 us

profile of v9, /device:TPU:0, one launch (start us, length us, event | category | flops | bytes accessed | tf_op | source)
XLA Modules:
  0.0 82.5 jit_solution(2100318361883251849)
XLA Ops:
  0.6 76.2 %shard_map.102 = (bf16[2048,2048]{1,0:T(8,128)(2,1)S(1)}, bf16[2048,640]{1,0:T(8,128)(2,1)S(1)}, bf16[2048,640]{1,0:T(8,128)(2,1)S(1)}, bf16[640,2048]{1,0:T(8,128)(2,1)S(1)}) custom-call(bf16[2048,2048]{1,0:T(8,128)(2,1)} %x_hbm.1, bf16[2048,2048]{1,0:T(8,128)(2,1)} %dy_hbm.1, bf16[2048,640]{1,0:T(8,128)(2,1)} %gate_hbm.1, bf16[2048,640]{1,0:T(8,128)(2,1)} %up_hbm.1, ...), custom_call_target="tpu_custom_call" | custom-call | tf_op jit(solution)/shard_map/pallas_call | solution.py:433
  76.8 5.7 %shard_map.103 = (bf16[2048,2048]{1,0:T(8,128)(2,1)}, bf16[2048,640]{1,0:T(8,128)(2,1)}, bf16[2048,640]{1,0:T(8,128)(2,1)}, bf16[640,2048]{1,0:T(8,128)(2,1)}) custom-call(bf16[2048,2048]{1,0:T(8,128)(2,1)S(1)} %get-tuple-element.8.dx, bf16[2048,640]{1,0:T(8,128)(2,1)S(1)} %get-tuple-element.9.dwg, bf16[2048,640]{1,0:T(8,128)(2,1)S(1)} %get-tuple-element.10.dwu, ...), custom_call_target="tpu_custom_call" | custom-call | tf_op jit(solution)/shard_map/pallas_call | solution.py:473
